TPU v7x, 32 devices: a whole 2x2x4 slice. The times are simulated.
32 devices in a mesh: lat: 16 (over z, y, x), ord: 2 (over core).
Axes of the slice: x: 2, y: 2, z: 4, core: 2. Of those that a mesh axis runs over, the one named last changes fastest.
Arguments:
- pressure: bfloat16 [2, 128, 5760], P(None, 'lat', 'ord'), may hold values from -6 to 6
- tables: bfloat16 [512, 128, 2048], P('ord', 'lat'), may hold values from -6 to 6
- quad_weight: float32 [128], replicated, may hold values from 0.5 to 2
- love_number: float32 [2048], replicated, may hold values from -0.5 to 0
- order_list: int32 [512], replicated, may hold values from 0 to 511, each once
- cycle_list: int32 [128], P('lat'), may hold values from 0 to 127, each once
Outputs:
- spectrum: float32 [2, 512, 2048], P(None, 'ord', 'lat')
- load_field: float32 [2, 128, 5760], P(None, 'lat', 'ord')
Inputs may be any that keep to these rules, and one draw needn't show every extreme that they name: `order_list`: every order from 0 to 511 stands in exactly one slot. `cycle_list`: every northern cycle from 0 to 127 stands in exactly one slot; the same slot of the southern half holds its mirror cycle.
All inputs are finite; a program needn't handle non-finite values.
Results may differ from a plain program's by a relative error of at most 0.0055.
Values may be sent and summed in bfloat16 or wider, within the bound.
A program may use at most 64 MiB of HBM per device.

v0:
```python
import functools
import math

import jax
import jax.numpy as jnp
import numpy as np
from jax import lax
from jax.experimental import pallas as pl
from jax.experimental.pallas import tpu as pltpu
from jax.sharding import PartitionSpec as P

DENSITY_RATIO = 3.0 * 1025.0 / 5517.0
LANES = 128
GROUPS = 8
STAGGER = 4
MESH = pl.DeviceIdType.MESH
NT = (((1,), (1,)), ((), ()))
F32 = jnp.float32
BF16 = jnp.bfloat16


def bit_orders(bits):
    base = list(range(bits))
    if bits < 3:
        return [base] * GROUPS
    a = base
    b = [1, 0] + base[2:]
    c = [2, 0, 1] + base[3:]
    d = [2, 1, 0] + base[3:]
    e = [0, 2, 1] + base[3:]
    f = [1, 2, 0] + base[3:]
    return [a, b, c, e, f, d, a, b]


def permuted(index, order):
    bits = len(order)
    return sum(((index // 2**b) % 2) * 2 ** (bits - 1 - at) for at, b in enumerate(order))


def twiddles(no, lon_local, orders):
    blocks = -(-lon_local // LANES)
    period = no * lon_local

    def turn(positions):
        phase = np.outer(positions, np.arange(orders)) % period
        angle = phase * (2.0 * math.pi / period)
        return np.cos(angle), np.sin(angle)

    fine = np.concatenate(turn(np.arange(LANES)), 1)
    high = fine.astype(BF16)
    low = (fine - high.astype(np.float64)).astype(BF16)
    starts = (lon_local * np.arange(no)[:, None] + LANES * np.arange(blocks)).reshape(-1)
    cos, sin = turn(starts)
    return np.concatenate([high, low], 0), cos.astype(np.float32), sin.astype(np.float32)


def kernel(
    n, no,
    press_hbm, tables_ref, quad_hbm, love_hbm, order_hbm, cycle_hbm, fine_hbm, cos_hbm, sin_hbm,
    spec_ref, field_ref,
    tab, press_ref, quad_ref, love_ref, order_ref, cycle_ref, fine, cos_q, sin_q,
    gathered, wide, partial, orders_ref, pick, lhs, part, landed, scaled,
    natural, rotated, out_signal, in_signal,
    tab_sem, in_sem, press_sem, rs_sem, ag_sem, field_sem,
):
    bits = n.bit_length() - 1
    me = lax.axis_index("lat")
    core = lax.axis_index("ord")
    cycles = press_ref.shape[1]
    lon_local = press_ref.shape[2]
    local_orders = orders_ref.shape[0]
    degrees = tables_ref.shape[1]
    share = degrees // n
    go = local_orders // GROUPS
    rows_g = go * cycles
    both = 2 * cycles
    blocks = max(1, min(n, 1024 // share))
    width = blocks * share
    orders_of = bit_orders(bits)
    period = lon_local * no
    turns = cos_q.shape[0] // no
    modes = order_ref.shape[1]

    barrier = pltpu.get_barrier_semaphore()
    partners = []
    for b in range(bits):
        mine = (me // 2**b) % 2
        partners.append(me + (1 - 2 * mine) * 2**b)
    peers = [lax.rem(core + i, no) for i in range(1, no)]
    for peer in peers:
        pl.semaphore_signal(barrier, inc=1, device_id=(me, peer), device_id_type=MESH)
    for partner in partners:
        pl.semaphore_signal(barrier, inc=1, device_id=(partner, core), device_id_type=MESH)

    loads = []
    pairs = (
        (press_hbm, press_ref), (order_hbm, order_ref), (quad_hbm, quad_ref), (cycle_hbm, cycle_ref),
        (fine_hbm, fine), (cos_hbm, cos_q), (sin_hbm, sin_q), (love_hbm, love_ref),
    )
    for i, (source, to) in enumerate(pairs):
        copy = pltpu.make_async_copy(source, to, in_sem.at[i])
        copy.start()
        loads.append(copy)
    tab_copies = []
    for g in range(GROUPS):
        rows = pl.ds(g * rows_g, rows_g)
        copy = pltpu.make_async_copy(tables_ref.at[rows], tab.at[rows], tab_sem.at[g])
        copy.start()
        tab_copies.append(copy)

    pl.semaphore_wait(barrier, bits + no - 1)
    loads[0].wait()
    press_copies = []
    for i, peer in enumerate(peers):
        copy = pltpu.make_async_remote_copy(
            src_ref=press_ref,
            dst_ref=gathered.at[i],
            send_sem=press_sem.at[0, i],
            recv_sem=press_sem.at[1, i],
            device_id=(me, peer),
            device_id_type=MESH,
        )
        copy.start()
        press_copies.append(copy)

    def widen(at, piece):
        for q in range(turns):
            first = q * LANES
            count = min(LANES, lon_local - first)
            rows = jnp.concatenate([piece[h, :, first : first + count].astype(F32) for h in range(2)], 0)
            if count < LANES:
                rows = jnp.concatenate([rows, jnp.zeros((both, LANES - count), F32)], 1)
            rows = rows.astype(BF16)
            wide[at, q * both : (q + 1) * both, :LANES] = rows
            wide[at, q * both : (q + 1) * both, LANES:] = rows

    def transform(at, origin, start):
        partial[...] = jnp.dot(wide[at], fine[...], preferred_element_type=F32)

        def turn(q, carry):
            cos_sum, sin_sum = carry
            rows = pl.ds(pl.multiple_of(q * both, both), both)
            c = partial[rows, :modes]
            s = partial[rows, modes:]
            cq = cos_q[pl.ds(origin * turns + q, 1), :]
            sq = sin_q[pl.ds(origin * turns + q, 1), :]
            return cos_sum + (cq * c - sq * s), sin_sum + (sq * c + cq * s)

        return lax.fori_loop(0, turns, turn, start)

    widen(0, press_ref)
    for copy in loads[1:]:
        copy.wait()
    shape = (local_orders, modes)
    slot = core * local_orders + lax.broadcasted_iota(jnp.int32, shape, 0)
    lane = lax.broadcasted_iota(jnp.int32, shape, 1)
    order_col = jnp.sum(
        jnp.where(slot == lane, order_ref[...].astype(F32), 0.0), axis=1, keepdims=True
    ).astype(jnp.int32)
    orders_ref[...] = order_col
    pick[...] = jnp.where(order_col == lane, 1.0, 0.0).astype(BF16)

    square = (cycles, cycles)
    eye = lax.broadcasted_iota(jnp.int32, square, 0) == lax.broadcasted_iota(jnp.int32, square, 1)
    cycle_col = jnp.sum(
        jnp.where(eye, cycle_ref[...].astype(F32), 0.0), axis=1, keepdims=True
    ).astype(jnp.int32)
    quad_lane = lax.broadcasted_iota(jnp.int32, (cycles, quad_ref.shape[1]), 1)
    weight = jnp.sum(jnp.where(quad_lane == cycle_col, quad_ref[...], 0.0), axis=1, keepdims=True)
    weight = weight * (1.0 / math.sqrt(quad_ref.shape[1])) * (1.0 / math.sqrt(period))

    col = lax.broadcasted_iota(jnp.int32, (go, rows_g), 1) // cycles
    row = lax.broadcasted_iota(jnp.int32, (go, rows_g), 0)
    diagonal = row == col
    spread_row = lax.broadcasted_iota(jnp.int32, (4 * cycles, 4 * rows_g), 0)
    spread_col = lax.broadcasted_iota(jnp.int32, (4 * cycles, 4 * rows_g), 1)
    spread = jnp.where(
        spread_row == (spread_col // rows_g) * cycles + spread_col % cycles, 1.0, 0.0
    ).astype(BF16)
    pick_row = lax.broadcasted_iota(jnp.int32, (cycles, rows_g), 0)
    pick_col = lax.broadcasted_iota(jnp.int32, (cycles, rows_g), 1)
    gather_rows = jnp.where(pick_row == pick_col % cycles, 1.0, 0.0).astype(BF16)

    zero = jnp.zeros((both, modes), F32)
    sums = transform(0, core, (zero, zero))
    for i, copy in enumerate(press_copies):
        copy.wait()
        widen(i + 1, gathered.at[i])
        sums = transform(i + 1, lax.rem(core + no - 1 - i, no), sums)
    cos_sum, sin_sum = sums
    folded = jnp.concatenate(
        [
            weight * (cos_sum[:cycles] + cos_sum[cycles:]),
            -weight * (sin_sum[:cycles] + sin_sum[cycles:]),
            weight * (cos_sum[:cycles] - cos_sum[cycles:]),
            -weight * (sin_sum[:cycles] - sin_sum[cycles:]),
        ],
        0,
    ).astype(BF16)
    chosen = lax.dot_general(pick[...], folded, NT, preferred_element_type=F32).astype(BF16)
    repeated = jnp.dot(chosen, spread, preferred_element_type=F32)
    for g in range(GROUPS):
        rows = repeated[g * go : (g + 1) * go]
        lhs[g] = jnp.concatenate(
            [jnp.where(diagonal, rows[:, c * rows_g : (c + 1) * rows_g], 0.0) for c in range(4)], 0
        ).astype(BF16)

    def parity(g, first):
        degree = first + lax.broadcasted_iota(jnp.int32, (go, width), 1)
        order = orders_ref[g * go : (g + 1) * go, :]
        return (degree + order) & 1 == 0, degree >= order

    def region(g, k):
        base = 0
        for at in range(k):
            base = base + ((me // 2 ** orders_of[g][at]) % 2) * (n >> (at + 1))
        return base

    def analyse(g):
        tab_copies[g].wait()
        left = lhs[g]
        for i in range(degrees // width):
            first = i * width
            product = jnp.dot(
                left, tab[g * rows_g : (g + 1) * rows_g, pl.ds(first, width)], preferred_element_type=F32
            )
            even, present = parity(g, first)
            real = jnp.where(present, jnp.where(even, product[:go], product[2 * go : 3 * go]), 0.0)
            imag = jnp.where(present, jnp.where(even, product[go : 2 * go], product[3 * go :]), 0.0)
            value = jnp.concatenate([real, imag], 0).astype(BF16)
            for j in range(blocks):
                to = permuted(i * blocks + j, orders_of[g])
                part[g, to] = value[:, j * share : (j + 1) * share]

    reduce_copies = {}
    gather_copies = {}

    def send_reduce(g, k):
        h = n >> (k + 1)
        b = orders_of[g][k]
        mine = (me // 2**b) % 2
        copy = pltpu.make_async_remote_copy(
            src_ref=part.at[g, pl.ds(region(g, k) + (1 - mine) * h, h)],
            dst_ref=landed.at[g, pl.ds(n - (n >> k), h)],
            send_sem=rs_sem.at[0, g, k],
            recv_sem=rs_sem.at[1, g, k],
            device_id=(partners[b], core),
            device_id_type=MESH,
        )
        copy.start()
        reduce_copies[g, k] = copy

    def take_reduce(g, k):
        h = n >> (k + 1)
        reduce_copies[g, k].wait_recv()
        keep = region(g, k + 1)
        off = n - (n >> k)
        if k < bits - 1:

            def add(i, carry):
                part[g, keep + i] = (
                    part[g, keep + i].astype(F32) + landed[g, off + i].astype(F32)
                ).astype(BF16)
                return carry

            lax.fori_loop(0, h, add, 0, unroll=min(h, 4))
            send_reduce(g, k + 1)
            return
        total = part[g, keep].astype(F32) + landed[g, off].astype(F32)
        spec_ref[0, g * go : (g + 1) * go, :] = total[:go]
        spec_ref[1, g * go : (g + 1) * go, :] = total[go:]
        scaled[g, keep] = (DENSITY_RATIO * (1.0 + love_ref[pl.ds(me, 1), :]) * total).astype(BF16)
        send_gather(g, bits - 1)

    def send_gather(g, k):
        h = n >> (k + 1)
        b = orders_of[g][k]
        mine = pl.ds(region(g, k + 1), h)
        copy = pltpu.make_async_remote_copy(
            src_ref=scaled.at[g, mine],
            dst_ref=scaled.at[g, mine],
            send_sem=ag_sem.at[0, g, k],
            recv_sem=ag_sem.at[1, g, k],
            device_id=(partners[b], core),
            device_id_type=MESH,
        )
        copy.start()
        gather_copies[g, k] = copy

    def take_gather(g, k):
        gather_copies[g, k].wait_recv()
        if k > 0:
            send_gather(g, k - 1)

    def synthesise(g):
        def chunk(i, total):
            first = pl.multiple_of(i * width, width)
            even, _ = parity(g, first)
            pieces = [scaled[g, permuted(i * blocks + j, orders_of[g])] for j in range(blocks)]
            both = jnp.concatenate(pieces, 1).astype(F32)
            real, imag = both[:go], both[go:]
            stacked = jnp.concatenate(
                [real, imag, jnp.where(even, real, -real), jnp.where(even, imag, -imag)], 0
            ).astype(BF16)
            return total + lax.dot_general(
                stacked, tab[g * rows_g : (g + 1) * rows_g, pl.ds(first, width)], NT,
                preferred_element_type=F32,
            )

        total = lax.fori_loop(0, degrees // width, chunk, jnp.zeros((4 * go, rows_g), F32))
        total = total * (1.0 / math.sqrt(degrees))
        signal = jnp.concatenate(
            [
                lax.dot_general(
                    gather_rows,
                    jnp.where(diagonal, total[c * go : (c + 1) * go], 0.0).astype(BF16),
                    NT, preferred_element_type=F32,
                )
                for c in range(4)
            ],
            0,
        )
        piece = jnp.dot(
            signal.astype(BF16), pick[g * go : (g + 1) * go, :], preferred_element_type=F32
        )
        natural[...] = piece if g == 0 else natural[...] + piece

    steps = []
    for g in range(GROUPS):
        steps.append((g, g, lambda g=g: (analyse(g), send_reduce(g, 0))))
        for k in range(bits):
            steps.append((g + STAGGER * (k + 1), g, lambda g=g, k=k: take_reduce(g, k)))
        for i, k in enumerate(reversed(range(bits))):
            steps.append((g + STAGGER * (bits + i + 1), g, lambda g=g, k=k: take_gather(g, k)))
        steps.append((g + STAGGER * 2 * bits + 0.5, g, lambda g=g: synthesise(g)))
    for _, _, step in sorted(steps, key=lambda s: (s[0], s[1])):
        step()

    out_signal[...] = natural[...].astype(BF16)
    field_copies = []
    for i, peer in enumerate(peers):
        copy = pltpu.make_async_remote_copy(
            src_ref=out_signal,
            dst_ref=in_signal.at[i],
            send_sem=field_sem.at[0, i],
            recv_sem=field_sem.at[1, i],
            device_id=(me, peer),
            device_id_type=MESH,
        )
        copy.start()
        field_copies.append(copy)
    total = out_signal[...].astype(F32)
    for i, copy in enumerate(field_copies):
        copy.wait_recv()
        total = total + in_signal[i].astype(F32)
    total = total * (1.0 / math.sqrt(modes))
    real = jnp.concatenate([total[:cycles], total[2 * cycles : 3 * cycles]], 0)
    imag = jnp.concatenate([total[cycles : 2 * cycles], total[3 * cycles :]], 0)
    for q in range(turns):
        cq = cos_q[pl.ds(core * turns + q, 1), :]
        sq = sin_q[pl.ds(core * turns + q, 1), :]
        rows = slice(q * both, (q + 1) * both)
        rotated[rows, :modes] = (real * cq - imag * sq).astype(BF16)
        rotated[rows, modes:] = (-real * sq - imag * cq).astype(BF16)
    parts = lax.dot_general(rotated[...], fine[...], NT, preferred_element_type=F32)
    field = parts[:, :LANES] + parts[:, LANES:]
    for q in range(turns):
        first = q * LANES
        count = min(LANES, lon_local - first)
        for h in range(2):
            at = q * both + h * cycles
            field_ref[h, :, first : first + count] = field[at : at + cycles, :count]
    for copy in list(reduce_copies.values()) + list(gather_copies.values()) + field_copies:
        copy.wait_send()


def finish(half_spec, half_field, spec_ref, field_ref):
    spec_ref[...] = half_spec[...]
    field_ref[...] = half_field[...]


def per_device(n, no, pressure, tables, quad_weight, love_number, order_list, cycle_list):
    _, cycles, lon_local = pressure.shape
    local_orders, _, degrees = tables.shape
    bits = n.bit_length() - 1
    share = degrees // n
    go = local_orders // GROUPS
    rows_g = go * cycles
    modes = order_list.shape[0]
    turns = -(-lon_local // LANES)
    fine, cos_q, sin_q = [jnp.asarray(table) for table in twiddles(no, lon_local, modes)]
    small = (
        quad_weight[None, :], love_number.reshape(n, share), order_list[None, :], cycle_list[None, :],
        fine, cos_q, sin_q,
    )
    vmem = pl.BlockSpec(memory_space=pltpu.VMEM)
    hbm = pl.BlockSpec(memory_space=pl.ANY)
    blocks = pltpu.VMEM((GROUPS, n, 2 * go, share), BF16)
    spectrum, field = pl.pallas_call(
        functools.partial(kernel, n, no),
        out_shape=(
            jax.ShapeDtypeStruct((2, local_orders, share), F32),
            jax.ShapeDtypeStruct((2, cycles, lon_local), F32),
        ),
        in_specs=[hbm] * 9,
        out_specs=(vmem, vmem),
        scratch_shapes=[
            pltpu.VMEM((local_orders * cycles, degrees), BF16),
            pltpu.VMEM((2, cycles, lon_local), BF16),
            *[pltpu.VMEM(array.shape, array.dtype) for array in small],
            pltpu.VMEM((no - 1, 2, cycles, lon_local), BF16),
            pltpu.VMEM((no, turns * 2 * cycles, 2 * LANES), BF16),
            pltpu.VMEM((turns * 2 * cycles, 2 * modes), F32),
            pltpu.VMEM((local_orders, 1), jnp.int32),
            pltpu.VMEM((local_orders, modes), BF16),
            pltpu.VMEM((GROUPS, 4 * go, rows_g), BF16),
            blocks, blocks, blocks,
            pltpu.VMEM((4 * cycles, modes), F32),
            pltpu.VMEM((turns * 2 * cycles, 2 * modes), BF16),
            pltpu.VMEM((4 * cycles, modes), BF16),
            pltpu.VMEM((no - 1, 4 * cycles, modes), BF16),
            pltpu.SemaphoreType.DMA((GROUPS,)),
            pltpu.SemaphoreType.DMA((8,)),
            pltpu.SemaphoreType.DMA((2, no - 1)),
            pltpu.SemaphoreType.DMA((2, GROUPS, bits)),
            pltpu.SemaphoreType.DMA((2, GROUPS, bits)),
            pltpu.SemaphoreType.DMA((2, no - 1)),
        ],
        compiler_params=pltpu.CompilerParams(
            collective_id=0, has_side_effects=True, vmem_limit_bytes=56 * 1024 * 1024
        ),
    )(pressure, tables.reshape(local_orders * cycles, degrees), *small)
    return pl.pallas_call(
        finish,
        out_shape=(
            jax.ShapeDtypeStruct(spectrum.shape, F32),
            jax.ShapeDtypeStruct(field.shape, F32),
        ),
        in_specs=[vmem, vmem],
        out_specs=(vmem, vmem),
    )(spectrum, field)


def solution(mesh):
    placed = (P(None, "lat", "ord"), P("ord", "lat", None), P(), P(), P(), P("lat"))
    return jax.shard_map(
        functools.partial(per_device, mesh.shape["lat"], mesh.shape["ord"]),
        mesh=mesh,
        in_specs=placed,
        out_specs=(P(None, "ord", "lat"), P(None, "lat", "ord")),
        check_vma=False,
    )
```

profile of v0, /device:TPU:1, one launch (start us, length us, event | category | flops | bytes accessed | tf_op | source)
XLA Modules:
  0.0 59.2 jit_solution(8931255180579873607)
XLA Ops:
  0.6 56.8 %shard_map.104 = (f32[2,256,128]{2,1,0:T(8,128)}, f32[2,8,2880]{2,1,0:T(8,128)}) custom-call(bf16[2,8,2880]{2,1,0:T(8,128)(2,1)} %press_hbm.1, bf16[2048,2048]{1,0:T(8,128)(2,1)} %bitcast.5, f32[1,128]{1,0:T(1,128)} %bitcast.8, f32[16,128]{1,0:T(8,128)} %bitcast.6, s32[1,512]{1,0:T(1,128)} %bitcast.7, s32[1,8]{1,0:T(1,128)} %bitcast.9, ...), custom_call_target="tpu_custom_call" | custom-call | tf_op jit(solution)/shard_map/pallas_call | solution.py:399
  57.4 1.8 %shard_map.105 = (f32[2,256,128]{2,1,0:T(8,128)}, f32[2,8,2880]{2,1,0:T(8,128)}) custom-call(f32[2,256,128]{2,1,0:T(8,128)} %get-tuple-element.4.half_spec, f32[2,8,2880]{2,1,0:T(8,128)} %get-tuple-element.5.half_field), custom_call_target="tpu_custom_call" | custom-call | tf_op jit(solution)/shard_map/pallas_call | solution.py:433
where the time goes:
time: 59.4 us; the launch traced here: 59.2 us
  Pallas kernels  58.6 us (99%)
  between operations  0.64 us (1%)
    pallas_call x1, Pallas kernels, per_device(): pl.pallas_call(functools.partial(kernel, n, no), out_shape=(jax.ShapeDtyp...  56.8 us
    pallas_call x1, Pallas kernels, per_device(): pl.pallas_call(finish, out_shape=(jax.ShapeDtypeStruct(spectrum.shape, F3...  1.78 us

commit v1 on v0

--- a/solution.py
+++ b/solution.py
@@ -11,7 +11,7 @@
 
 DENSITY_RATIO = 3.0 * 1025.0 / 5517.0
 LANES = 128
-GROUPS = 8
+UNITS = 8
 STAGGER = 4
 MESH = pl.DeviceIdType.MESH
 NT = (((1,), (1,)), ((), ()))
@@ -19,17 +19,40 @@
 BF16 = jnp.bfloat16
 
 
-def bit_orders(bits):
+PLAN_ORDERS = (
+    (1, 3, 0, 2), (2, 0, 1, 3), (1, 2, 0, 3), (0, 1, 2, 3), (1, 0, 3, 2), (0, 2, 1, 3),
+    (1, 0, 3, 2), (2, 1, 3, 0), (0, 2, 1, 3), (0, 2, 1, 3), (2, 0, 1, 3), (2, 3, 0, 1),
+    (2, 0, 1, 3), (1, 0, 2, 3), (0, 1, 2, 3), (1, 0, 3, 2),
+)
+PLAN_STEPS = (
+    192, 224, 96, 160, 128, 209, 193, 0, 32, 97, 241, 64, 210, 129, 1, 177, 145, 194, 225, 49, 17,
+    33, 113, 65, 98, 242, 195, 161, 130, 211, 226, 50, 146, 81, 2, 34, 18, 178, 114, 66, 162, 243,
+    131, 212, 196, 51, 227, 147, 3, 99, 35, 19, 82, 163, 115, 179, 244, 67, 132, 213, 197, 100, 83,
+    52, 4, 148, 36, 228, 116, 20, 164, 180, 245, 214, 198, 133, 68, 101, 5, 84, 117, 53, 149, 37,
+    181, 229, 21, 165, 134, 69, 215, 246, 6, 102, 85, 54, 22, 38, 150, 230, 118, 247, 182, 135, 166,
+    86, 199, 103, 216, 70, 7, 55, 231, 151, 23, 119, 136, 39, 183, 217, 248, 137, 71, 167, 87, 249,
+    104, 105, 56, 57, 8, 9, 200, 232, 201, 233, 24, 25, 152, 153, 40, 120, 41, 121, 184, 185, 72,
+    73, 168, 88, 89, 169,
+)
+
+
+def plan(bits):
+    if bits == len(PLAN_ORDERS[0]):
+        return [list(order) for order in PLAN_ORDERS], [divmod(code, 16) for code in PLAN_STEPS]
     base = list(range(bits))
-    if bits < 3:
-        return [base] * GROUPS
-    a = base
-    b = [1, 0] + base[2:]
-    c = [2, 0, 1] + base[3:]
-    d = [2, 1, 0] + base[3:]
-    e = [0, 2, 1] + base[3:]
-    f = [1, 2, 0] + base[3:]
-    return [a, b, c, e, f, d, a, b]
+    orders = [base]
+    if bits >= 3:
+        a, b, c, d, e, f = [
+            list(head) + base[3:]
+            for head in ((0, 1, 2), (1, 0, 2), (2, 0, 1), (2, 1, 0), (0, 2, 1), (1, 2, 0))
+        ]
+        orders = [a, b, c, e, f, d, a, b]
+    orders = [orders[g % len(orders)] for g in range(UNITS)]
+    steps = [(g - UNITS, g, 0) for g in range(UNITS)]
+    for g in range(UNITS):
+        steps += [(g + STAGGER * i, g, i) for i in range(1, 2 * bits + 1)]
+        steps.append((g + STAGGER * 2 * bits + 0.5, g, 2 * bits + 1))
+    return orders, [(g, i) for _, g, i in sorted(steps)]
 
 
 def permuted(index, order):
@@ -66,17 +89,21 @@
     bits = n.bit_length() - 1
     me = lax.axis_index("lat")
     core = lax.axis_index("ord")
+    orders_of, steps = plan(bits)
+    groups = len(orders_of)
+    per_unit = groups // UNITS
     cycles = press_ref.shape[1]
     lon_local = press_ref.shape[2]
     local_orders = orders_ref.shape[0]
     degrees = tables_ref.shape[1]
     share = degrees // n
-    go = local_orders // GROUPS
+    go = local_orders // groups
     rows_g = go * cycles
+    uo = local_orders // UNITS
+    rows_u = uo * cycles
     both = 2 * cycles
     blocks = max(1, min(n, 1024 // share))
     width = blocks * share
-    orders_of = bit_orders(bits)
     period = lon_local * no
     turns = cos_q.shape[0] // no
     modes = order_ref.shape[1]
@@ -101,15 +128,8 @@
         copy = pltpu.make_async_copy(source, to, in_sem.at[i])
         copy.start()
         loads.append(copy)
-    tab_copies = []
-    for g in range(GROUPS):
-        rows = pl.ds(g * rows_g, rows_g)
-        copy = pltpu.make_async_copy(tables_ref.at[rows], tab.at[rows], tab_sem.at[g])
-        copy.start()
-        tab_copies.append(copy)
-
+    loads[0].wait()
     pl.semaphore_wait(barrier, bits + no - 1)
-    loads[0].wait()
     press_copies = []
     for i, peer in enumerate(peers):
         copy = pltpu.make_async_remote_copy(
@@ -137,20 +157,26 @@
     def transform(at, origin, start):
         partial[...] = jnp.dot(wide[at], fine[...], preferred_element_type=F32)
 
-        def turn(q, carry):
-            cos_sum, sin_sum = carry
-            rows = pl.ds(pl.multiple_of(q * both, both), both)
+        cos_sum, sin_sum = start
+        for q in range(turns):
+            rows = slice(q * both, (q + 1) * both)
             c = partial[rows, :modes]
             s = partial[rows, modes:]
             cq = cos_q[pl.ds(origin * turns + q, 1), :]
             sq = sin_q[pl.ds(origin * turns + q, 1), :]
-            return cos_sum + (cq * c - sq * s), sin_sum + (sq * c + cq * s)
-
-        return lax.fori_loop(0, turns, turn, start)
+            cos_sum = cos_sum + (cq * c - sq * s)
+            sin_sum = sin_sum + (sq * c + cq * s)
+        return cos_sum, sin_sum
 
     widen(0, press_ref)
     for copy in loads[1:]:
         copy.wait()
+    tab_copies = []
+    for u in range(UNITS):
+        rows = pl.ds(u * rows_u, rows_u)
+        copy = pltpu.make_async_copy(tables_ref.at[rows], tab.at[rows], tab_sem.at[u])
+        copy.start()
+        tab_copies.append(copy)
     shape = (local_orders, modes)
     slot = core * local_orders + lax.broadcasted_iota(jnp.int32, shape, 0)
     lane = lax.broadcasted_iota(jnp.int32, shape, 1)
@@ -169,17 +195,16 @@
     weight = jnp.sum(jnp.where(quad_lane == cycle_col, quad_ref[...], 0.0), axis=1, keepdims=True)
     weight = weight * (1.0 / math.sqrt(quad_ref.shape[1])) * (1.0 / math.sqrt(period))
 
-    col = lax.broadcasted_iota(jnp.int32, (go, rows_g), 1) // cycles
-    row = lax.broadcasted_iota(jnp.int32, (go, rows_g), 0)
+    col = lax.broadcasted_iota(jnp.int32, (uo, rows_u), 1) // cycles
+    row = lax.broadcasted_iota(jnp.int32, (uo, rows_u), 0)
     diagonal = row == col
-    spread_row = lax.broadcasted_iota(jnp.int32, (4 * cycles, 4 * rows_g), 0)
-    spread_col = lax.broadcasted_iota(jnp.int32, (4 * cycles, 4 * rows_g), 1)
+    spread_row = lax.broadcasted_iota(jnp.int32, (4 * cycles, 4 * rows_u), 0)
+    spread_col = lax.broadcasted_iota(jnp.int32, (4 * cycles, 4 * rows_u), 1)
     spread = jnp.where(
-        spread_row == (spread_col // rows_g) * cycles + spread_col % cycles, 1.0, 0.0
+        spread_row == (spread_col // rows_u) * cycles + spread_col % cycles, 1.0, 0.0
     ).astype(BF16)
-    pick_row = lax.broadcasted_iota(jnp.int32, (cycles, rows_g), 0)
-    pick_col = lax.broadcasted_iota(jnp.int32, (cycles, rows_g), 1)
-    gather_rows = jnp.where(pick_row == pick_col % cycles, 1.0, 0.0).astype(BF16)
+    lane_order = lax.broadcasted_iota(jnp.int32, (cycles, 4 * go), 1) % go
+    lane_part = lax.broadcasted_iota(jnp.int32, (cycles, 4 * go), 1) // go
 
     zero = jnp.zeros((both, modes), F32)
     sums = transform(0, core, (zero, zero))
@@ -199,15 +224,15 @@
     ).astype(BF16)
     chosen = lax.dot_general(pick[...], folded, NT, preferred_element_type=F32).astype(BF16)
     repeated = jnp.dot(chosen, spread, preferred_element_type=F32)
-    for g in range(GROUPS):
-        rows = repeated[g * go : (g + 1) * go]
-        lhs[g] = jnp.concatenate(
-            [jnp.where(diagonal, rows[:, c * rows_g : (c + 1) * rows_g], 0.0) for c in range(4)], 0
+    for u in range(UNITS):
+        rows = repeated[u * uo : (u + 1) * uo]
+        lhs[u] = jnp.concatenate(
+            [jnp.where(diagonal, rows[:, c * rows_u : (c + 1) * rows_u], 0.0) for c in range(4)], 0
         ).astype(BF16)
 
-    def parity(g, first):
-        degree = first + lax.broadcasted_iota(jnp.int32, (go, width), 1)
-        order = orders_ref[g * go : (g + 1) * go, :]
+    def parity(start, count, first):
+        degree = first + lax.broadcasted_iota(jnp.int32, (count, width), 1)
+        order = orders_ref[start : start + count, :]
         return (degree + order) & 1 == 0, degree >= order
 
     def region(g, k):
@@ -216,21 +241,25 @@
             base = base + ((me // 2 ** orders_of[g][at]) % 2) * (n >> (at + 1))
         return base
 
-    def analyse(g):
-        tab_copies[g].wait()
-        left = lhs[g]
+    def analyse(u):
+        tab_copies[u].wait()
+        left = lhs[u]
         for i in range(degrees // width):
             first = i * width
             product = jnp.dot(
-                left, tab[g * rows_g : (g + 1) * rows_g, pl.ds(first, width)], preferred_element_type=F32
+                left, tab[u * rows_u : (u + 1) * rows_u, first : first + width],
+                preferred_element_type=F32,
             )
-            even, present = parity(g, first)
-            real = jnp.where(present, jnp.where(even, product[:go], product[2 * go : 3 * go]), 0.0)
-            imag = jnp.where(present, jnp.where(even, product[go : 2 * go], product[3 * go :]), 0.0)
-            value = jnp.concatenate([real, imag], 0).astype(BF16)
-            for j in range(blocks):
-                to = permuted(i * blocks + j, orders_of[g])
-                part[g, to] = value[:, j * share : (j + 1) * share]
+            even, present = parity(u * uo, uo, first)
+            real = jnp.where(present, jnp.where(even, product[:uo], product[2 * uo : 3 * uo]), 0.0)
+            imag = jnp.where(present, jnp.where(even, product[uo : 2 * uo], product[3 * uo :]), 0.0)
+            for v in range(per_unit):
+                g = u * per_unit + v
+                rows = slice(v * go, (v + 1) * go)
+                value = jnp.concatenate([real[rows], imag[rows]], 0).astype(BF16)
+                for j in range(blocks):
+                    to = permuted(i * blocks + j, orders_of[g])
+                    part[g, to] = value[:, j * share : (j + 1) * share]
 
     reduce_copies = {}
     gather_copies = {}
@@ -293,48 +322,41 @@
             send_gather(g, k - 1)
 
     def synthesise(g):
-        def chunk(i, total):
-            first = pl.multiple_of(i * width, width)
-            even, _ = parity(g, first)
+        total = jnp.zeros((rows_g, 4 * go), F32)
+        for i in range(degrees // width):
+            first = i * width
+            even, _ = parity(g * go, go, first)
             pieces = [scaled[g, permuted(i * blocks + j, orders_of[g])] for j in range(blocks)]
-            both = jnp.concatenate(pieces, 1).astype(F32)
-            real, imag = both[:go], both[go:]
+            both_parts = jnp.concatenate(pieces, 1).astype(F32)
+            real, imag = both_parts[:go], both_parts[go:]
             stacked = jnp.concatenate(
                 [real, imag, jnp.where(even, real, -real), jnp.where(even, imag, -imag)], 0
             ).astype(BF16)
-            return total + lax.dot_general(
-                stacked, tab[g * rows_g : (g + 1) * rows_g, pl.ds(first, width)], NT,
+            total = total + lax.dot_general(
+                tab[g * rows_g : (g + 1) * rows_g, first : first + width], stacked, NT,
                 preferred_element_type=F32,
             )
-
-        total = lax.fori_loop(0, degrees // width, chunk, jnp.zeros((4 * go, rows_g), F32))
-        total = total * (1.0 / math.sqrt(degrees))
-        signal = jnp.concatenate(
-            [
-                lax.dot_general(
-                    gather_rows,
-                    jnp.where(diagonal, total[c * go : (c + 1) * go], 0.0).astype(BF16),
-                    NT, preferred_element_type=F32,
-                )
-                for c in range(4)
-            ],
-            0,
-        )
-        piece = jnp.dot(
-            signal.astype(BF16), pick[g * go : (g + 1) * go, :], preferred_element_type=F32
-        )
-        natural[...] = piece if g == 0 else natural[...] + piece
-
-    steps = []
-    for g in range(GROUPS):
-        steps.append((g, g, lambda g=g: (analyse(g), send_reduce(g, 0))))
-        for k in range(bits):
-            steps.append((g + STAGGER * (k + 1), g, lambda g=g, k=k: take_reduce(g, k)))
-        for i, k in enumerate(reversed(range(bits))):
-            steps.append((g + STAGGER * (bits + i + 1), g, lambda g=g, k=k: take_gather(g, k)))
-        steps.append((g + STAGGER * 2 * bits + 0.5, g, lambda g=g: synthesise(g)))
-    for _, _, step in sorted(steps, key=lambda s: (s[0], s[1])):
-        step()
+        signal = jnp.zeros((cycles, 4 * go), F32)
+        for o in range(go):
+            signal = jnp.where(lane_order == o, total[o * cycles : (o + 1) * cycles], signal)
+        signal = signal * (1.0 / math.sqrt(degrees))
+        split = jnp.concatenate([jnp.where(lane_part == c, signal, 0.0) for c in range(4)], 0)
+        chosen_rows = jnp.concatenate([pick[g * go : (g + 1) * go, :]] * 4, 0)
+        piece = jnp.dot(split.astype(BF16), chosen_rows, preferred_element_type=F32)
+        natural[...] += piece
+
+    natural[...] = jnp.zeros_like(natural)
+    for g, i in steps:
+        if i == 0:
+            analyse(g // per_unit)
+            for v in range(per_unit):
+                send_reduce(g + v, 0)
+        elif i <= bits:
+            take_reduce(g, i - 1)
+        elif i <= 2 * bits:
+            take_gather(g, 2 * bits - i)
+        else:
+            synthesise(g)
 
     out_signal[...] = natural[...].astype(BF16)
     field_copies = []
@@ -384,8 +406,9 @@
     local_orders, _, degrees = tables.shape
     bits = n.bit_length() - 1
     share = degrees // n
-    go = local_orders // GROUPS
-    rows_g = go * cycles
+    groups = len(plan(bits)[0])
+    go = local_orders // groups
+    uo = local_orders // UNITS
     modes = order_list.shape[0]
     turns = -(-lon_local // LANES)
     fine, cos_q, sin_q = [jnp.asarray(table) for table in twiddles(no, lon_local, modes)]
@@ -395,7 +418,7 @@
     )
     vmem = pl.BlockSpec(memory_space=pltpu.VMEM)
     hbm = pl.BlockSpec(memory_space=pl.ANY)
-    blocks = pltpu.VMEM((GROUPS, n, 2 * go, share), BF16)
+    blocks = pltpu.VMEM((groups, n, 2 * go, share), BF16)
     spectrum, field = pl.pallas_call(
         functools.partial(kernel, n, no),
         out_shape=(
@@ -413,17 +436,17 @@
             pltpu.VMEM((turns * 2 * cycles, 2 * modes), F32),
             pltpu.VMEM((local_orders, 1), jnp.int32),
             pltpu.VMEM((local_orders, modes), BF16),
-            pltpu.VMEM((GROUPS, 4 * go, rows_g), BF16),
+            pltpu.VMEM((UNITS, 4 * uo, uo * cycles), BF16),
             blocks, blocks, blocks,
             pltpu.VMEM((4 * cycles, modes), F32),
             pltpu.VMEM((turns * 2 * cycles, 2 * modes), BF16),
             pltpu.VMEM((4 * cycles, modes), BF16),
             pltpu.VMEM((no - 1, 4 * cycles, modes), BF16),
-            pltpu.SemaphoreType.DMA((GROUPS,)),
+            pltpu.SemaphoreType.DMA((UNITS,)),
             pltpu.SemaphoreType.DMA((8,)),
             pltpu.SemaphoreType.DMA((2, no - 1)),
-            pltpu.SemaphoreType.DMA((2, GROUPS, bits)),
-            pltpu.SemaphoreType.DMA((2, GROUPS, bits)),
+            pltpu.SemaphoreType.DMA((2, groups, bits)),
+            pltpu.SemaphoreType.DMA((2, groups, bits)),
             pltpu.SemaphoreType.DMA((2, no - 1)),
         ],
         compiler_params=pltpu.CompilerParams(

time: 59.4 us -> 56.9 us (0.958)
  Pallas kernels: 58.6 us -> 56.1 us
    pallas_call x1, Pallas kernels: 56.8 us -> 54.3 us  [per_device(): pl.pallas_call(functools.partial(kernel, n, no), out_shape=(jax.ShapeDtyp...]
where the time goes in v1:
time: 56.9 us; the launch traced here: 56.7 us
  Pallas kernels  56.1 us (99%)
  between operations  0.64 us (1%)
    pallas_call x1, Pallas kernels, per_device(): pl.pallas_call(functools.partial(kernel, n, no), out_shape=(jax.ShapeDtyp...  54.3 us
    pallas_call x1, Pallas kernels, per_device(): pl.pallas_call(finish, out_shape=(jax.ShapeDtypeStruct(spectrum.shape, F3...  1.78 us

profile of v1, /device:TPU:1, one launch (start us, length us, event | category | flops | bytes accessed | tf_op | source)
XLA Modules:
  0.0 56.7 jit_solution(4165188348635001525)
XLA Ops:
  0.6 54.3 %shard_map.104 = (f32[2,256,128]{2,1,0:T(8,128)}, f32[2,8,2880]{2,1,0:T(8,128)}) custom-call(bf16[2,8,2880]{2,1,0:T(8,128)(2,1)} %press_hbm.1, bf16[2048,2048]{1,0:T(8,128)(2,1)} %bitcast.5, f32[1,128]{1,0:T(1,128)} %bitcast.8, f32[16,128]{1,0:T(8,128)} %bitcast.6, s32[1,512]{1,0:T(1,128)} %bitcast.7, s32[1,8]{1,0:T(1,128)} %bitcast.9, ...), custom_call_target="tpu_custom_call" | custom-call | tf_op jit(solution)/shard_map/pallas_call | solution.py:422
  54.9 1.8 %shard_map.105 = (f32[2,256,128]{2,1,0:T(8,128)}, f32[2,8,2880]{2,1,0:T(8,128)}) custom-call(f32[2,256,128]{2,1,0:T(8,128)} %get-tuple-element.4.half_spec, f32[2,8,2880]{2,1,0:T(8,128)} %get-tuple-element.5.half_field), custom_call_target="tpu_custom_call" | custom-call | tf_op jit(solution)/shard_map/pallas_call | solution.py:456

commit v2 on v1

--- a/solution.py
+++ b/solution.py
@@ -20,19 +20,19 @@
 
 
 PLAN_ORDERS = (
-    (1, 3, 0, 2), (2, 0, 1, 3), (1, 2, 0, 3), (0, 1, 2, 3), (1, 0, 3, 2), (0, 2, 1, 3),
-    (1, 0, 3, 2), (2, 1, 3, 0), (0, 2, 1, 3), (0, 2, 1, 3), (2, 0, 1, 3), (2, 3, 0, 1),
-    (2, 0, 1, 3), (1, 0, 2, 3), (0, 1, 2, 3), (1, 0, 3, 2),
+    (1, 0, 2, 3), (2, 0, 1, 3), (2, 0, 3, 1), (0, 2, 1, 3), (2, 3, 1, 0), (0, 1, 2, 3),
+    (0, 1, 2, 3), (1, 0, 2, 3), (0, 1, 2, 3), (1, 0, 2, 3), (2, 1, 0, 3), (2, 0, 1, 3),
+    (2, 1, 0, 3), (1, 0, 2, 3), (0, 1, 2, 3), (1, 3, 2, 0),
 )
 PLAN_STEPS = (
-    192, 224, 96, 160, 128, 209, 193, 0, 32, 97, 241, 64, 210, 129, 1, 177, 145, 194, 225, 49, 17,
-    33, 113, 65, 98, 242, 195, 161, 130, 211, 226, 50, 146, 81, 2, 34, 18, 178, 114, 66, 162, 243,
-    131, 212, 196, 51, 227, 147, 3, 99, 35, 19, 82, 163, 115, 179, 244, 67, 132, 213, 197, 100, 83,
-    52, 4, 148, 36, 228, 116, 20, 164, 180, 245, 214, 198, 133, 68, 101, 5, 84, 117, 53, 149, 37,
-    181, 229, 21, 165, 134, 69, 215, 246, 6, 102, 85, 54, 22, 38, 150, 230, 118, 247, 182, 135, 166,
-    86, 199, 103, 216, 70, 7, 55, 231, 151, 23, 119, 136, 39, 183, 217, 248, 137, 71, 167, 87, 249,
-    104, 105, 56, 57, 8, 9, 200, 232, 201, 233, 24, 25, 152, 153, 40, 120, 41, 121, 184, 185, 72,
-    73, 168, 88, 89, 169,
+    32, 224, 128, 160, 192, 225, 145, 161, 64, 129, 49, 209, 96, 226, 241, 33, 146, 0, 130, 210, 65,
+    193, 81, 50, 162, 97, 177, 227, 113, 34, 1, 147, 163, 131, 17, 194, 242, 82, 98, 114, 211, 66,
+    228, 178, 35, 51, 2, 195, 164, 18, 243, 83, 132, 67, 148, 115, 179, 99, 212, 229, 244, 52, 3,
+    19, 196, 165, 84, 133, 149, 36, 116, 68, 100, 230, 180, 213, 245, 20, 4, 197, 53, 37, 85, 134,
+    150, 117, 69, 101, 166, 181, 214, 231, 246, 198, 5, 21, 54, 86, 38, 135, 70, 102, 167, 118, 215,
+    182, 247, 199, 6, 151, 22, 232, 233, 55, 39, 87, 71, 103, 136, 137, 216, 119, 217, 183, 168,
+    169, 248, 7, 249, 23, 200, 201, 152, 153, 56, 57, 40, 41, 88, 89, 72, 73, 104, 105, 120, 121,
+    184, 185, 8, 9, 24, 25,
 )
 
 
@@ -83,7 +83,7 @@
     spec_ref, field_ref,
     tab, press_ref, quad_ref, love_ref, order_ref, cycle_ref, fine, cos_q, sin_q,
     gathered, wide, partial, orders_ref, pick, lhs, part, landed, scaled,
-    natural, rotated, out_signal, in_signal,
+    signals, rotated, out_signal, in_signal,
     tab_sem, in_sem, press_sem, rs_sem, ag_sem, field_sem,
 ):
     bits = n.bit_length() - 1
@@ -171,12 +171,12 @@
     widen(0, press_ref)
     for copy in loads[1:]:
         copy.wait()
-    tab_copies = []
-    for u in range(UNITS):
+    tab_copies = {}
+    for u in [g // per_unit for g, i in steps if i == 0]:
         rows = pl.ds(u * rows_u, rows_u)
         copy = pltpu.make_async_copy(tables_ref.at[rows], tab.at[rows], tab_sem.at[u])
         copy.start()
-        tab_copies.append(copy)
+        tab_copies[u] = copy
     shape = (local_orders, modes)
     slot = core * local_orders + lax.broadcasted_iota(jnp.int32, shape, 0)
     lane = lax.broadcasted_iota(jnp.int32, shape, 1)
@@ -204,7 +204,6 @@
         spread_row == (spread_col // rows_u) * cycles + spread_col % cycles, 1.0, 0.0
     ).astype(BF16)
     lane_order = lax.broadcasted_iota(jnp.int32, (cycles, 4 * go), 1) % go
-    lane_part = lax.broadcasted_iota(jnp.int32, (cycles, 4 * go), 1) // go
 
     zero = jnp.zeros((both, modes), F32)
     sums = transform(0, core, (zero, zero))
@@ -340,12 +339,9 @@
         for o in range(go):
             signal = jnp.where(lane_order == o, total[o * cycles : (o + 1) * cycles], signal)
         signal = signal * (1.0 / math.sqrt(degrees))
-        split = jnp.concatenate([jnp.where(lane_part == c, signal, 0.0) for c in range(4)], 0)
-        chosen_rows = jnp.concatenate([pick[g * go : (g + 1) * go, :]] * 4, 0)
-        piece = jnp.dot(split.astype(BF16), chosen_rows, preferred_element_type=F32)
-        natural[...] += piece
-
-    natural[...] = jnp.zeros_like(natural)
+        for c in range(4):
+            signals[c * cycles : (c + 1) * cycles, g * go : (g + 1) * go] = signal[:, c * go : (c + 1) * go]
+
     for g, i in steps:
         if i == 0:
             analyse(g // per_unit)
@@ -358,7 +354,8 @@
         else:
             synthesise(g)
 
-    out_signal[...] = natural[...].astype(BF16)
+    natural = jnp.dot(signals[...].astype(BF16), pick[...], preferred_element_type=F32)
+    out_signal[...] = natural.astype(BF16)
     field_copies = []
     for i, peer in enumerate(peers):
         copy = pltpu.make_async_remote_copy(
@@ -371,7 +368,7 @@
         )
         copy.start()
         field_copies.append(copy)
-    total = out_signal[...].astype(F32)
+    total = natural
     for i, copy in enumerate(field_copies):
         copy.wait_recv()
         total = total + in_signal[i].astype(F32)
@@ -438,7 +435,7 @@
             pltpu.VMEM((local_orders, modes), BF16),
             pltpu.VMEM((UNITS, 4 * uo, uo * cycles), BF16),
             blocks, blocks, blocks,
-            pltpu.VMEM((4 * cycles, modes), F32),
+            pltpu.VMEM((4 * cycles, local_orders), F32),
             pltpu.VMEM((turns * 2 * cycles, 2 * modes), BF16),
             pltpu.VMEM((4 * cycles, modes), BF16),
             pltpu.VMEM((no - 1, 4 * cycles, modes), BF16),

time: 56.9 us -> 56.4 us (level)
  no operation moved by 1% of the time
where the time goes in v2:
time: 56.4 us; the launch traced here: 56.3 us
  Pallas kernels  55.6 us (99%)
  between operations  0.64 us (1%)
    pallas_call x1, Pallas kernels, per_device(): pl.pallas_call(functools.partial(kernel, n, no), out_shape=(jax.ShapeDtyp...  53.9 us
    pallas_call x1, Pallas kernels, per_device(): pl.pallas_call(finish, out_shape=(jax.ShapeDtypeStruct(spectrum.shape, F3...  1.78 us

profile of v2, /device:TPU:1, one launch (start us, length us, event | category | flops | bytes accessed | tf_op | source)
XLA Modules:
  0.0 56.3 jit_solution(11896639069049333479)
XLA Ops:
  0.6 53.9 %shard_map.104 = (f32[2,256,128]{2,1,0:T(8,128)}, f32[2,8,2880]{2,1,0:T(8,128)}) custom-call(bf16[2,8,2880]{2,1,0:T(8,128)(2,1)} %press_hbm.1, bf16[2048,2048]{1,0:T(8,128)(2,1)} %bitcast.5, f32[1,128]{1,0:T(1,128)} %bitcast.8, f32[16,128]{1,0:T(8,128)} %bitcast.6, s32[1,512]{1,0:T(1,128)} %bitcast.7, s32[1,8]{1,0:T(1,128)} %bitcast.9, ...), custom_call_target="tpu_custom_call" | custom-call | tf_op jit(solution)/shard_map/pallas_call | solution.py:419
  54.5 1.8 %shard_map.105 = (f32[2,256,128]{2,1,0:T(8,128)}, f32[2,8,2880]{2,1,0:T(8,128)}) custom-call(f32[2,256,128]{2,1,0:T(8,128)} %get-tuple-element.4.half_spec, f32[2,8,2880]{2,1,0:T(8,128)} %get-tuple-element.5.half_field), custom_call_target="tpu_custom_call" | custom-call | tf_op jit(solution)/shard_map/pallas_call | solution.py:453

commit v3 on v2

--- a/solution.py
+++ b/solution.py
@@ -80,11 +80,11 @@
 def kernel(
     n, no,
     press_hbm, tables_ref, quad_hbm, love_hbm, order_hbm, cycle_hbm, fine_hbm, cos_hbm, sin_hbm,
-    spec_ref, field_ref,
+    spec_hbm, field_hbm,
     tab, press_ref, quad_ref, love_ref, order_ref, cycle_ref, fine, cos_q, sin_q,
     gathered, wide, partial, orders_ref, pick, lhs, part, landed, scaled,
-    signals, rotated, out_signal, in_signal,
-    tab_sem, in_sem, press_sem, rs_sem, ag_sem, field_sem,
+    spec_ref, field_ref, signals, rotated, out_signal, in_signal,
+    tab_sem, in_sem, spec_sem, press_sem, send_sem, hop_sem, field_sem,
 ):
     bits = n.bit_length() - 1
     me = lax.axis_index("lat")
@@ -270,8 +270,8 @@
         copy = pltpu.make_async_remote_copy(
             src_ref=part.at[g, pl.ds(region(g, k) + (1 - mine) * h, h)],
             dst_ref=landed.at[g, pl.ds(n - (n >> k), h)],
-            send_sem=rs_sem.at[0, g, k],
-            recv_sem=rs_sem.at[1, g, k],
+            send_sem=send_sem.at[0],
+            recv_sem=hop_sem.at[g, k],
             device_id=(partners[b], core),
             device_id_type=MESH,
         )
@@ -307,8 +307,8 @@
         copy = pltpu.make_async_remote_copy(
             src_ref=scaled.at[g, mine],
             dst_ref=scaled.at[g, mine],
-            send_sem=ag_sem.at[0, g, k],
-            recv_sem=ag_sem.at[1, g, k],
+            send_sem=send_sem.at[1],
+            recv_sem=hop_sem.at[g, (k - 1) % (bits + 1)],
             device_id=(partners[b], core),
             device_id_type=MESH,
         )
@@ -321,7 +321,7 @@
             send_gather(g, k - 1)
 
     def synthesise(g):
-        total = jnp.zeros((rows_g, 4 * go), F32)
+        signal = jnp.zeros((cycles, 4 * go), F32)
         for i in range(degrees // width):
             first = i * width
             even, _ = parity(g * go, go, first)
@@ -331,18 +331,23 @@
             stacked = jnp.concatenate(
                 [real, imag, jnp.where(even, real, -real), jnp.where(even, imag, -imag)], 0
             ).astype(BF16)
-            total = total + lax.dot_general(
+            total = lax.dot_general(
                 tab[g * rows_g : (g + 1) * rows_g, first : first + width], stacked, NT,
                 preferred_element_type=F32,
             )
-        signal = jnp.zeros((cycles, 4 * go), F32)
-        for o in range(go):
-            signal = jnp.where(lane_order == o, total[o * cycles : (o + 1) * cycles], signal)
+            piece = jnp.zeros((cycles, 4 * go), F32)
+            for o in range(go):
+                piece = jnp.where(lane_order == o, total[o * cycles : (o + 1) * cycles], piece)
+            signal = signal + piece
         signal = signal * (1.0 / math.sqrt(degrees))
         for c in range(4):
             signals[c * cycles : (c + 1) * cycles, g * go : (g + 1) * go] = signal[:, c * go : (c + 1) * go]
 
-    for g, i in steps:
+    spec_copy = pltpu.make_async_copy(spec_ref, spec_hbm, spec_sem.at[0])
+    last_sum = max(at for at, (_, i) in enumerate(steps) if i == bits)
+    for at, (g, i) in enumerate(steps):
+        if at == last_sum + 1:
+            spec_copy.start()
         if i == 0:
             analyse(g // per_unit)
             for v in range(per_unit):
@@ -389,8 +394,15 @@
         for h in range(2):
             at = q * both + h * cycles
             field_ref[h, :, first : first + count] = field[at : at + cycles, :count]
-    for copy in list(reduce_copies.values()) + list(gather_copies.values()) + field_copies:
+    field_copy = pltpu.make_async_copy(field_ref, field_hbm, spec_sem.at[1])
+    field_copy.start()
+    for i, blocks_ref in enumerate((part, scaled)):
+        sent = blocks_ref.at[:, pl.ds(0, n - 1)]
+        pltpu.make_async_copy(sent, sent, send_sem.at[i]).wait()
+    for copy in field_copies:
         copy.wait_send()
+    spec_copy.wait()
+    field_copy.wait()
 
 
 def finish(half_spec, half_field, spec_ref, field_ref):
@@ -423,7 +435,7 @@
             jax.ShapeDtypeStruct((2, cycles, lon_local), F32),
         ),
         in_specs=[hbm] * 9,
-        out_specs=(vmem, vmem),
+        out_specs=(hbm, hbm),
         scratch_shapes=[
             pltpu.VMEM((local_orders * cycles, degrees), BF16),
             pltpu.VMEM((2, cycles, lon_local), BF16),
@@ -435,15 +447,18 @@
             pltpu.VMEM((local_orders, modes), BF16),
             pltpu.VMEM((UNITS, 4 * uo, uo * cycles), BF16),
             blocks, blocks, blocks,
+            pltpu.VMEM((2, local_orders, share), F32),
+            pltpu.VMEM((2, cycles, lon_local), F32),
             pltpu.VMEM((4 * cycles, local_orders), F32),
             pltpu.VMEM((turns * 2 * cycles, 2 * modes), BF16),
             pltpu.VMEM((4 * cycles, modes), BF16),
             pltpu.VMEM((no - 1, 4 * cycles, modes), BF16),
             pltpu.SemaphoreType.DMA((UNITS,)),
             pltpu.SemaphoreType.DMA((8,)),
+            pltpu.SemaphoreType.DMA((2,)),
             pltpu.SemaphoreType.DMA((2, no - 1)),
-            pltpu.SemaphoreType.DMA((2, groups, bits)),
-            pltpu.SemaphoreType.DMA((2, groups, bits)),
+            pltpu.SemaphoreType.DMA((2,)),
+            pltpu.SemaphoreType.DMA((groups, bits + 1)),
             pltpu.SemaphoreType.DMA((2, no - 1)),
         ],
         compiler_params=pltpu.CompilerParams(

time: 56.4 us -> 52.8 us (0.936)
  Pallas kernels: 55.6 us -> 52 us
    pallas_call x1, Pallas kernels: 53.9 us -> 50.2 us  [per_device(): pl.pallas_call(functools.partial(kernel, n, no), out_shape=(jax.ShapeDtyp...]
where the time goes in v3:
time: 52.8 us; the launch traced here: 52.6 us
  Pallas kernels  52 us (98%)
  between operations  0.64 us (1%)
    pallas_call x1, Pallas kernels, per_device(): pl.pallas_call(functools.partial(kernel, n, no), out_shape=(jax.ShapeDtyp...  50.2 us
    pallas_call x1, Pallas kernels, per_device(): pl.pallas_call(finish, out_shape=(jax.ShapeDtypeStruct(spectrum.shape, F3...  1.78 us

profile of v3, /device:TPU:1, one launch (start us, length us, event | category | flops | bytes accessed | tf_op | source)
XLA Modules:
  0.0 52.6 jit_solution(4698692518850478491)
XLA Ops:
  0.6 50.2 %shard_map.104 = (f32[2,256,128]{2,1,0:T(8,128)}, f32[2,8,2880]{2,1,0:T(8,128)}) custom-call(bf16[2,8,2880]{2,1,0:T(8,128)(2,1)} %press_hbm.1, bf16[2048,2048]{1,0:T(8,128)(2,1)} %bitcast.5, f32[1,128]{1,0:T(1,128)} %bitcast.8, f32[16,128]{1,0:T(8,128)} %bitcast.6, s32[1,512]{1,0:T(1,128)} %bitcast.7, s32[1,8]{1,0:T(1,128)} %bitcast.9, ...), custom_call_target="tpu_custom_call" | custom-call | tf_op jit(solution)/shard_map/pallas_call | solution.py:431
  50.8 1.8 %shard_map.105 = (f32[2,256,128]{2,1,0:T(8,128)}, f32[2,8,2880]{2,1,0:T(8,128)}) custom-call(f32[2,256,128]{2,1,0:T(8,128)} %get-tuple-element.4.half_spec, f32[2,8,2880]{2,1,0:T(8,128)} %get-tuple-element.5.half_field), custom_call_target="tpu_custom_call" | custom-call | tf_op jit(solution)/shard_map/pallas_call | solution.py:468

commit v4 on v3

--- a/solution.py
+++ b/solution.py
@@ -20,19 +20,19 @@
 
 
 PLAN_ORDERS = (
-    (1, 0, 2, 3), (2, 0, 1, 3), (2, 0, 3, 1), (0, 2, 1, 3), (2, 3, 1, 0), (0, 1, 2, 3),
-    (0, 1, 2, 3), (1, 0, 2, 3), (0, 1, 2, 3), (1, 0, 2, 3), (2, 1, 0, 3), (2, 0, 1, 3),
-    (2, 1, 0, 3), (1, 0, 2, 3), (0, 1, 2, 3), (1, 3, 2, 0),
+    (1, 3, 0, 2), (2, 1, 0, 3), (2, 0, 1, 3), (0, 1, 2, 3), (1, 0, 2, 3), (0, 1, 3, 2),
+    (1, 0, 2, 3), (2, 3, 1, 0), (0, 2, 1, 3), (0, 1, 2, 3), (2, 0, 1, 3), (1, 0, 3, 2),
+    (2, 0, 1, 3), (1, 2, 0, 3), (0, 1, 2, 3), (2, 1, 0, 3),
 )
 PLAN_STEPS = (
-    32, 224, 128, 160, 192, 225, 145, 161, 64, 129, 49, 209, 96, 226, 241, 33, 146, 0, 130, 210, 65,
-    193, 81, 50, 162, 97, 177, 227, 113, 34, 1, 147, 163, 131, 17, 194, 242, 82, 98, 114, 211, 66,
-    228, 178, 35, 51, 2, 195, 164, 18, 243, 83, 132, 67, 148, 115, 179, 99, 212, 229, 244, 52, 3,
-    19, 196, 165, 84, 133, 149, 36, 116, 68, 100, 230, 180, 213, 245, 20, 4, 197, 53, 37, 85, 134,
-    150, 117, 69, 101, 166, 181, 214, 231, 246, 198, 5, 21, 54, 86, 38, 135, 70, 102, 167, 118, 215,
-    182, 247, 199, 6, 151, 22, 232, 233, 55, 39, 87, 71, 103, 136, 137, 216, 119, 217, 183, 168,
-    169, 248, 7, 249, 23, 200, 201, 152, 153, 56, 57, 40, 41, 88, 89, 72, 73, 104, 105, 120, 121,
-    184, 185, 8, 9, 24, 25,
+    160, 64, 96, 128, 0, 161, 81, 32, 113, 224, 145, 129, 162, 97, 17, 1, 177, 33, 192, 225, 163,
+    65, 241, 146, 18, 82, 130, 98, 178, 49, 209, 2, 34, 114, 226, 193, 66, 164, 19, 242, 147, 99,
+    83, 131, 35, 115, 179, 3, 50, 210, 227, 67, 243, 194, 84, 148, 165, 100, 20, 211, 36, 4, 116,
+    180, 195, 228, 132, 68, 244, 51, 166, 149, 101, 21, 85, 5, 37, 181, 117, 196, 212, 133, 69, 229,
+    245, 150, 52, 6, 22, 102, 86, 38, 167, 134, 197, 246, 213, 182, 230, 151, 70, 53, 103, 87, 118,
+    198, 7, 247, 135, 54, 214, 183, 168, 169, 39, 23, 231, 152, 153, 71, 104, 105, 119, 88, 89, 199,
+    8, 9, 248, 55, 249, 136, 215, 137, 184, 185, 232, 40, 233, 41, 72, 24, 25, 73, 120, 121, 200,
+    201, 56, 57, 216, 217,
 )
 
 
@@ -55,6 +55,35 @@
     return orders, [(g, i) for _, g, i in sorted(steps)]
 
 
+def shared_slots(bits, orders, steps):
+    per_unit = len(orders) // UNITS
+    take, send = {}, {}
+    for at, (g, i) in enumerate(steps):
+        if i == 0:
+            send.update({(g + v, 0): at for v in range(per_unit)})
+        elif i <= 2 * bits:
+            take[g, i - 1] = at
+            send[g, i] = at
+
+    def along(message):
+        g, hop = message
+        return orders[g][min(hop, 2 * bits - 1 - hop)]
+
+    free_after, slots = [], {}
+    for message in sorted(take, key=lambda m: (send[m], m)):
+        known = max(
+            (send[m] for m in take if along(m) == along(message) and take[m] <= send[message]),
+            default=-1,
+        )
+        fits = [s for s, at in enumerate(free_after) if at <= known]
+        slot = max(fits, key=lambda s: free_after[s]) if fits else len(free_after)
+        if not fits:
+            free_after.append(0)
+        free_after[slot] = take[message]
+        slots[message] = slot
+    return slots
+
+
 def permuted(index, order):
     bits = len(order)
     return sum(((index // 2**b) % 2) * 2 ** (bits - 1 - at) for at, b in enumerate(order))
@@ -74,15 +103,16 @@
     low = (fine - high.astype(np.float64)).astype(BF16)
     starts = (lon_local * np.arange(no)[:, None] + LANES * np.arange(blocks)).reshape(-1)
     cos, sin = turn(starts)
-    return np.concatenate([high, low], 0), cos.astype(np.float32), sin.astype(np.float32)
+    fine = np.concatenate([high, low], 0)
+    return fine, cos.astype(np.float32), sin.astype(np.float32), np.ascontiguousarray(fine.T)
 
 
 def kernel(
     n, no,
-    press_hbm, tables_ref, quad_hbm, love_hbm, order_hbm, cycle_hbm, fine_hbm, cos_hbm, sin_hbm,
+    press_hbm, tables_ref, quad_hbm, love_hbm, order_hbm, cycle_hbm, fine_hbm, cos_hbm, sin_hbm, back_hbm,
     spec_hbm, field_hbm,
-    tab, press_ref, quad_ref, love_ref, order_ref, cycle_ref, fine, cos_q, sin_q,
-    gathered, wide, partial, orders_ref, pick, lhs, part, landed, scaled,
+    tab, press_ref, quad_ref, love_ref, order_ref, cycle_ref, fine, cos_q, sin_q, back,
+    gathered, wide, partial, orders_ref, pick, repeated, part, landed, scaled,
     spec_ref, field_ref, signals, rotated, out_signal, in_signal,
     tab_sem, in_sem, spec_sem, press_sem, send_sem, hop_sem, field_sem,
 ):
@@ -90,6 +120,7 @@
     me = lax.axis_index("lat")
     core = lax.axis_index("ord")
     orders_of, steps = plan(bits)
+    slots = shared_slots(bits, orders_of, steps)
     groups = len(orders_of)
     per_unit = groups // UNITS
     cycles = press_ref.shape[1]
@@ -177,6 +208,8 @@
         copy = pltpu.make_async_copy(tables_ref.at[rows], tab.at[rows], tab_sem.at[u])
         copy.start()
         tab_copies[u] = copy
+    back_copy = pltpu.make_async_copy(back_hbm, back, in_sem.at[8])
+    back_copy.start()
     shape = (local_orders, modes)
     slot = core * local_orders + lax.broadcasted_iota(jnp.int32, shape, 0)
     lane = lax.broadcasted_iota(jnp.int32, shape, 1)
@@ -222,13 +255,7 @@
         0,
     ).astype(BF16)
     chosen = lax.dot_general(pick[...], folded, NT, preferred_element_type=F32).astype(BF16)
-    repeated = jnp.dot(chosen, spread, preferred_element_type=F32)
-    for u in range(UNITS):
-        rows = repeated[u * uo : (u + 1) * uo]
-        lhs[u] = jnp.concatenate(
-            [jnp.where(diagonal, rows[:, c * rows_u : (c + 1) * rows_u], 0.0) for c in range(4)], 0
-        ).astype(BF16)
-
+    repeated[...] = jnp.dot(chosen, spread, preferred_element_type=F32)
     def parity(start, count, first):
         degree = first + lax.broadcasted_iota(jnp.int32, (count, width), 1)
         order = orders_ref[start : start + count, :]
@@ -242,7 +269,10 @@
 
     def analyse(u):
         tab_copies[u].wait()
-        left = lhs[u]
+        rows = repeated[u * uo : (u + 1) * uo, :]
+        left = jnp.concatenate(
+            [jnp.where(diagonal, rows[:, c * rows_u : (c + 1) * rows_u], 0.0) for c in range(4)], 0
+        ).astype(BF16)
         for i in range(degrees // width):
             first = i * width
             product = jnp.dot(
@@ -271,7 +301,7 @@
             src_ref=part.at[g, pl.ds(region(g, k) + (1 - mine) * h, h)],
             dst_ref=landed.at[g, pl.ds(n - (n >> k), h)],
             send_sem=send_sem.at[0],
-            recv_sem=hop_sem.at[g, k],
+            recv_sem=hop_sem.at[slots[g, k]],
             device_id=(partners[b], core),
             device_id_type=MESH,
         )
@@ -308,7 +338,7 @@
             src_ref=scaled.at[g, mine],
             dst_ref=scaled.at[g, mine],
             send_sem=send_sem.at[1],
-            recv_sem=hop_sem.at[g, (k - 1) % (bits + 1)],
+            recv_sem=hop_sem.at[slots[g, 2 * bits - 1 - k]],
             device_id=(partners[b], core),
             device_id_type=MESH,
         )
@@ -359,6 +389,7 @@
         else:
             synthesise(g)
 
+    back_copy.wait()
     natural = jnp.dot(signals[...].astype(BF16), pick[...], preferred_element_type=F32)
     out_signal[...] = natural.astype(BF16)
     field_copies = []
@@ -386,7 +417,7 @@
         rows = slice(q * both, (q + 1) * both)
         rotated[rows, :modes] = (real * cq - imag * sq).astype(BF16)
         rotated[rows, modes:] = (-real * sq - imag * cq).astype(BF16)
-    parts = lax.dot_general(rotated[...], fine[...], NT, preferred_element_type=F32)
+    parts = jnp.dot(rotated[...], back[...], preferred_element_type=F32)
     field = parts[:, :LANES] + parts[:, LANES:]
     for q in range(turns):
         first = q * LANES
@@ -405,9 +436,17 @@
     field_copy.wait()
 
 
-def finish(half_spec, half_field, spec_ref, field_ref):
-    spec_ref[...] = half_spec[...]
-    field_ref[...] = half_field[...]
+def finish(half_spec, half_field, spec_ref, field_ref, spec, field, sems):
+    pairs = ((half_spec, spec, spec_ref), (half_field, field, field_ref))
+    loads = [pltpu.make_async_copy(a, b, sems.at[0, i]) for i, (a, b, _) in enumerate(pairs)]
+    stores = [pltpu.make_async_copy(b, c, sems.at[1, i]) for i, (_, b, c) in enumerate(pairs)]
+    for load in loads:
+        load.start()
+    for load, store in zip(loads, stores):
+        load.wait()
+        store.start()
+    for store in stores:
+        store.wait()
 
 
 def per_device(n, no, pressure, tables, quad_weight, love_number, order_list, cycle_list):
@@ -420,12 +459,11 @@
     uo = local_orders // UNITS
     modes = order_list.shape[0]
     turns = -(-lon_local // LANES)
-    fine, cos_q, sin_q = [jnp.asarray(table) for table in twiddles(no, lon_local, modes)]
+    fine, cos_q, sin_q, back = [jnp.asarray(table) for table in twiddles(no, lon_local, modes)]
     small = (
         quad_weight[None, :], love_number.reshape(n, share), order_list[None, :], cycle_list[None, :],
-        fine, cos_q, sin_q,
+        fine, cos_q, sin_q, back,
     )
-    vmem = pl.BlockSpec(memory_space=pltpu.VMEM)
     hbm = pl.BlockSpec(memory_space=pl.ANY)
     blocks = pltpu.VMEM((groups, n, 2 * go, share), BF16)
     spectrum, field = pl.pallas_call(
@@ -434,7 +472,7 @@
             jax.ShapeDtypeStruct((2, local_orders, share), F32),
             jax.ShapeDtypeStruct((2, cycles, lon_local), F32),
         ),
-        in_specs=[hbm] * 9,
+        in_specs=[hbm] * 10,
         out_specs=(hbm, hbm),
         scratch_shapes=[
             pltpu.VMEM((local_orders * cycles, degrees), BF16),
@@ -445,7 +483,7 @@
             pltpu.VMEM((turns * 2 * cycles, 2 * modes), F32),
             pltpu.VMEM((local_orders, 1), jnp.int32),
             pltpu.VMEM((local_orders, modes), BF16),
-            pltpu.VMEM((UNITS, 4 * uo, uo * cycles), BF16),
+            pltpu.VMEM((local_orders, 4 * uo * cycles), F32),
             blocks, blocks, blocks,
             pltpu.VMEM((2, local_orders, share), F32),
             pltpu.VMEM((2, cycles, lon_local), F32),
@@ -454,11 +492,11 @@
             pltpu.VMEM((4 * cycles, modes), BF16),
             pltpu.VMEM((no - 1, 4 * cycles, modes), BF16),
             pltpu.SemaphoreType.DMA((UNITS,)),
-            pltpu.SemaphoreType.DMA((8,)),
+            pltpu.SemaphoreType.DMA((9,)),
             pltpu.SemaphoreType.DMA((2,)),
             pltpu.SemaphoreType.DMA((2, no - 1)),
             pltpu.SemaphoreType.DMA((2,)),
-            pltpu.SemaphoreType.DMA((groups, bits + 1)),
+            pltpu.SemaphoreType.DMA((max(shared_slots(bits, *plan(bits)).values()) + 1,)),
             pltpu.SemaphoreType.DMA((2, no - 1)),
         ],
         compiler_params=pltpu.CompilerParams(
@@ -471,8 +509,13 @@
             jax.ShapeDtypeStruct(spectrum.shape, F32),
             jax.ShapeDtypeStruct(field.shape, F32),
         ),
-        in_specs=[vmem, vmem],
-        out_specs=(vmem, vmem),
+        in_specs=[hbm, hbm],
+        out_specs=(hbm, hbm),
+        scratch_shapes=[
+            pltpu.VMEM(spectrum.shape, F32),
+            pltpu.VMEM(field.shape, F32),
+            pltpu.SemaphoreType.DMA((2, 2)),
+        ],
     )(spectrum, field)
 
 

time: 52.8 us -> 52 us (0.985)
  Pallas kernels: 52 us -> 51.2 us
    pallas_call x1, Pallas kernels: 50.2 us -> 49.4 us  [per_device(): pl.pallas_call(functools.partial(kernel, n, no), out_shape=(jax.ShapeDtyp...]
where the time goes in v4:
time: 52 us; the launch traced here: 51.8 us
  Pallas kernels  51.2 us (98%)
  between operations  0.64 us (1%)
    pallas_call x1, Pallas kernels, per_device(): pl.pallas_call(functools.partial(kernel, n, no), out_shape=(jax.ShapeDtyp...  49.4 us
    pallas_call x1, Pallas kernels, per_device(): pl.pallas_call(finish, out_shape=(jax.ShapeDtypeStruct(spectrum.shape, F3...  1.74 us

profile of v4, /device:TPU:1, one launch (start us, length us, event | category | flops | bytes accessed | tf_op | source)
XLA Modules:
  0.0 51.8 jit_solution(492017413113379189)
XLA Ops:
  0.6 49.4 %shard_map.113 = (f32[2,256,128]{2,1,0:T(8,128)}, f32[2,8,2880]{2,1,0:T(8,128)}) custom-call(bf16[2,8,2880]{2,1,0:T(8,128)(2,1)} %press_hbm.1, bf16[2048,2048]{1,0:T(8,128)(2,1)} %bitcast.5, f32[1,128]{1,0:T(1,128)} %bitcast.8, f32[16,128]{1,0:T(8,128)} %bitcast.6, s32[1,512]{1,0:T(1,128)} %bitcast.7, s32[1,8]{1,0:T(1,128)} %bitcast.9, ...), custom_call_target="tpu_custom_call" | custom-call | tf_op jit(solution)/shard_map/pallas_call | solution.py:469
  50.1 1.7 %shard_map.114 = (f32[2,256,128]{2,1,0:T(8,128)}, f32[2,8,2880]{2,1,0:T(8,128)}) custom-call(f32[2,256,128]{2,1,0:T(8,128)} %get-tuple-element.4.half_spec, f32[2,8,2880]{2,1,0:T(8,128)} %get-tuple-element.5.half_field), custom_call_target="tpu_custom_call" | custom-call | tf_op jit(solution)/shard_map/pallas_call | solution.py:506

commit v5 on v4

--- a/solution.py
+++ b/solution.py
@@ -20,19 +20,20 @@
 
 
 PLAN_ORDERS = (
-    (1, 3, 0, 2), (2, 1, 0, 3), (2, 0, 1, 3), (0, 1, 2, 3), (1, 0, 2, 3), (0, 1, 3, 2),
-    (1, 0, 2, 3), (2, 3, 1, 0), (0, 2, 1, 3), (0, 1, 2, 3), (2, 0, 1, 3), (1, 0, 3, 2),
-    (2, 0, 1, 3), (1, 2, 0, 3), (0, 1, 2, 3), (2, 1, 0, 3),
+    (1, 2, 0, 3), (1, 0, 2, 3), (1, 2, 0, 3), (2, 0, 1, 3), (2, 0, 1, 3), (0, 3, 1, 2),
+    (2, 0, 1, 3), (1, 0, 2, 3), (0, 1, 2, 3), (0, 1, 2, 3), (1, 0, 3, 2), (1, 0, 3, 2),
+    (1, 0, 2, 3), (0, 3, 1, 2), (2, 3, 1, 0), (2, 0, 1, 3),
 )
 PLAN_STEPS = (
-    160, 64, 96, 128, 0, 161, 81, 32, 113, 224, 145, 129, 162, 97, 17, 1, 177, 33, 192, 225, 163,
-    65, 241, 146, 18, 82, 130, 98, 178, 49, 209, 2, 34, 114, 226, 193, 66, 164, 19, 242, 147, 99,
-    83, 131, 35, 115, 179, 3, 50, 210, 227, 67, 243, 194, 84, 148, 165, 100, 20, 211, 36, 4, 116,
-    180, 195, 228, 132, 68, 244, 51, 166, 149, 101, 21, 85, 5, 37, 181, 117, 196, 212, 133, 69, 229,
-    245, 150, 52, 6, 22, 102, 86, 38, 167, 134, 197, 246, 213, 182, 230, 151, 70, 53, 103, 87, 118,
-    198, 7, 247, 135, 54, 214, 183, 168, 169, 39, 23, 231, 152, 153, 71, 104, 105, 119, 88, 89, 199,
-    8, 9, 248, 55, 249, 136, 215, 137, 184, 185, 232, 40, 233, 41, 72, 24, 25, 73, 120, 121, 200,
-    201, 56, 57, 216, 217,
+    96, 192, 32, 64, 97, 113, 160, 224, 193, 128, 98, 209, 0, 81, 114, 49, 177, 33, 99, 225, 161,
+    65, 145, 241, 1, 129, 82, 50, 194, 34, 178, 210, 115, 162, 17, 146, 130, 100, 226, 66, 2, 242,
+    51, 195, 83, 35, 179, 18, 147, 131, 227, 3, 116, 101, 163, 84, 211, 67, 243, 36, 180, 52, 19,
+    196, 228, 148, 132, 4, 117, 212, 164, 85, 102, 68, 181, 244, 37, 53, 20, 197, 149, 5, 133, 118,
+    213, 229, 165, 38, 86, 69, 182, 245, 198, 21, 150, 6, 134, 54, 119, 230, 122, 166, 70, 214, 39,
+    246, 183, 22, 186, 42, 103, 151, 87, 90, 199, 55, 106, 58, 135, 7, 154, 202, 231, 234, 10, 247,
+    167, 120, 71, 215, 218, 121, 250, 23, 40, 138, 41, 26, 184, 104, 152, 185, 105, 74, 153, 200,
+    56, 88, 57, 201, 89, 170, 8, 232, 136, 9, 137, 233, 216, 168, 248, 169, 217, 249, 24, 72, 73,
+    25,
 )
 
 
@@ -52,6 +53,7 @@
     for g in range(UNITS):
         steps += [(g + STAGGER * i, g, i) for i in range(1, 2 * bits + 1)]
         steps.append((g + STAGGER * 2 * bits + 0.5, g, 2 * bits + 1))
+        steps.append((g + STAGGER * (2 * bits - 1) + 0.5, g, 2 * bits + 2))
     return orders, [(g, i) for _, g, i in sorted(steps)]
 
 
@@ -112,7 +114,7 @@
     press_hbm, tables_ref, quad_hbm, love_hbm, order_hbm, cycle_hbm, fine_hbm, cos_hbm, sin_hbm, back_hbm,
     spec_hbm, field_hbm,
     tab, press_ref, quad_ref, love_ref, order_ref, cycle_ref, fine, cos_q, sin_q, back,
-    gathered, wide, partial, orders_ref, pick, repeated, part, landed, scaled,
+    gathered, wide, partial, orders_ref, sign_rows, pick, repeated, part, landed, scaled,
     spec_ref, field_ref, signals, rotated, out_signal, in_signal,
     tab_sem, in_sem, spec_sem, press_sem, send_sem, hop_sem, field_sem,
 ):
@@ -236,6 +238,8 @@
     spread = jnp.where(
         spread_row == (spread_col // rows_u) * cycles + spread_col % cycles, 1.0, 0.0
     ).astype(BF16)
+    lane_parity = (order_col + lax.broadcasted_iota(jnp.int32, (local_orders, LANES), 1)) & 1
+    sign_rows[...] = jnp.where(lane_parity == 0, 1.0, -1.0)
     lane_order = lax.broadcasted_iota(jnp.int32, (cycles, 4 * go), 1) % go
 
     zero = jnp.zeros((both, modes), F32)
@@ -350,29 +354,62 @@
         if k > 0:
             send_gather(g, k - 1)
 
-    def synthesise(g):
+    def slots_of(g, total):
+        piece = jnp.zeros((cycles, 4 * go), F32)
+        for o in range(go):
+            piece = jnp.where(lane_order == o, total[o * cycles : (o + 1) * cycles], piece)
+        return piece
+
+    def keep_signal(g, signal, first):
+        signal = signal * (1.0 / math.sqrt(degrees))
+        for c in range(4):
+            at = slice(c * cycles, (c + 1) * cycles), slice(g * go, (g + 1) * go)
+            piece = signal[:, c * go : (c + 1) * go]
+            signals[at] = piece if first else signals[at] + piece
+
+    def stacked_of(pieces, signs):
+        both_parts = jnp.concatenate(pieces, 1).astype(F32)
+        real, imag = both_parts[:go], both_parts[go:]
+        return jnp.concatenate([real, imag, real * signs, imag * signs], 0).astype(BF16)
+
+    def synthesise_whole(g):
         signal = jnp.zeros((cycles, 4 * go), F32)
         for i in range(degrees // width):
             first = i * width
             even, _ = parity(g * go, go, first)
             pieces = [scaled[g, permuted(i * blocks + j, orders_of[g])] for j in range(blocks)]
-            both_parts = jnp.concatenate(pieces, 1).astype(F32)
-            real, imag = both_parts[:go], both_parts[go:]
-            stacked = jnp.concatenate(
-                [real, imag, jnp.where(even, real, -real), jnp.where(even, imag, -imag)], 0
-            ).astype(BF16)
+            stacked = stacked_of(pieces, jnp.where(even, 1.0, -1.0))
             total = lax.dot_general(
                 tab[g * rows_g : (g + 1) * rows_g, first : first + width], stacked, NT,
                 preferred_element_type=F32,
             )
-            piece = jnp.zeros((cycles, 4 * go), F32)
-            for o in range(go):
-                piece = jnp.where(lane_order == o, total[o * cycles : (o + 1) * cycles], piece)
-            signal = signal + piece
-        signal = signal * (1.0 / math.sqrt(degrees))
-        for c in range(4):
-            signals[c * cycles : (c + 1) * cycles, g * go : (g + 1) * go] = signal[:, c * go : (c + 1) * go]
-
+            signal = signal + slots_of(g, total)
+        keep_signal(g, signal, True)
+
+    def synthesise_half(g, late):
+        order = orders_of[g]
+        mine = (me // 2 ** order[0]) % 2
+        side = 1 - mine if late else mine
+        half = n // 2
+        quarter = half // 2
+        signs = jnp.concatenate([sign_rows[g * go : (g + 1) * go, :]] * (quarter * share // LANES), 1)
+        signal = jnp.zeros((cycles, 4 * go), F32)
+        for part_at in range(2):
+            pieces, columns = [], []
+            for i in range(part_at * quarter, (part_at + 1) * quarter):
+                block = side * 2 ** order[0]
+                for at in range(1, bits):
+                    block = block + ((i >> (bits - 1 - at)) & 1) * 2 ** order[at]
+                pieces.append(scaled[g, side * half + i])
+                start = pl.multiple_of(block * share, share)
+                columns.append(tab[g * rows_g : (g + 1) * rows_g, pl.ds(start, share)])
+            total = lax.dot_general(
+                jnp.concatenate(columns, 1), stacked_of(pieces, signs), NT, preferred_element_type=F32
+            )
+            signal = signal + slots_of(g, total)
+        keep_signal(g, signal, not late)
+
+    halves = share % LANES == 0 and n >= 4
     spec_copy = pltpu.make_async_copy(spec_ref, spec_hbm, spec_sem.at[0])
     last_sum = max(at for at, (_, i) in enumerate(steps) if i == bits)
     for at, (g, i) in enumerate(steps):
@@ -386,8 +423,11 @@
             take_reduce(g, i - 1)
         elif i <= 2 * bits:
             take_gather(g, 2 * bits - i)
+        elif not halves:
+            if i == 2 * bits + 1:
+                synthesise_whole(g)
         else:
-            synthesise(g)
+            synthesise_half(g, i == 2 * bits + 1)
 
     back_copy.wait()
     natural = jnp.dot(signals[...].astype(BF16), pick[...], preferred_element_type=F32)
@@ -482,6 +522,7 @@
             pltpu.VMEM((no, turns * 2 * cycles, 2 * LANES), BF16),
             pltpu.VMEM((turns * 2 * cycles, 2 * modes), F32),
             pltpu.VMEM((local_orders, 1), jnp.int32),
+            pltpu.VMEM((local_orders, LANES), F32),
             pltpu.VMEM((local_orders, modes), BF16),
             pltpu.VMEM((local_orders, 4 * uo * cycles), F32),
             blocks, blocks, blocks,

time: 52 us -> 50.9 us (0.979)
  Pallas kernels: 51.2 us -> 50.1 us
    pallas_call x1, Pallas kernels: 49.4 us -> 48.3 us  [per_device(): pl.pallas_call(functools.partial(kernel, n, no), out_shape=(jax.ShapeDtyp...]
where the time goes in v5:
time: 50.9 us; the launch traced here: 50.7 us
  Pallas kernels  50.1 us (98%)
  between operations  0.64 us (1%)
    pallas_call x1, Pallas kernels, per_device(): pl.pallas_call(functools.partial(kernel, n, no), out_shape=(jax.ShapeDtyp...  48.3 us
    pallas_call x1, Pallas kernels, per_device(): pl.pallas_call(finish, out_shape=(jax.ShapeDtypeStruct(spectrum.shape, F3...  1.74 us

profile of v5, /device:TPU:1, one launch (start us, length us, event | category | flops | bytes accessed | tf_op | source)
XLA Modules:
  0.0 50.7 jit_solution(1476540997084369977)
XLA Ops:
  0.6 48.3 %shard_map.113 = (f32[2,256,128]{2,1,0:T(8,128)}, f32[2,8,2880]{2,1,0:T(8,128)}) custom-call(bf16[2,8,2880]{2,1,0:T(8,128)(2,1)} %press_hbm.1, bf16[2048,2048]{1,0:T(8,128)(2,1)} %bitcast.5, f32[1,128]{1,0:T(1,128)} %bitcast.8, f32[16,128]{1,0:T(8,128)} %bitcast.6, s32[1,512]{1,0:T(1,128)} %bitcast.7, s32[1,8]{1,0:T(1,128)} %bitcast.9, ...), custom_call_target="tpu_custom_call" | custom-call | tf_op jit(solution)/shard_map/pallas_call | solution.py:509
  49.0 1.7 %shard_map.114 = (f32[2,256,128]{2,1,0:T(8,128)}, f32[2,8,2880]{2,1,0:T(8,128)}) custom-call(f32[2,256,128]{2,1,0:T(8,128)} %get-tuple-element.4.half_spec, f32[2,8,2880]{2,1,0:T(8,128)} %get-tuple-element.5.half_field), custom_call_target="tpu_custom_call" | custom-call | tf_op jit(solution)/shard_map/pallas_call | solution.py:547

commit v6 on v5

--- a/solution.py
+++ b/solution.py
@@ -20,20 +20,19 @@
 
 
 PLAN_ORDERS = (
-    (1, 2, 0, 3), (1, 0, 2, 3), (1, 2, 0, 3), (2, 0, 1, 3), (2, 0, 1, 3), (0, 3, 1, 2),
-    (2, 0, 1, 3), (1, 0, 2, 3), (0, 1, 2, 3), (0, 1, 2, 3), (1, 0, 3, 2), (1, 0, 3, 2),
-    (1, 0, 2, 3), (0, 3, 1, 2), (2, 3, 1, 0), (2, 0, 1, 3),
+    (0, 2, 1, 3), (2, 0, 1, 3), (0, 1, 3, 2), (0, 1, 3, 2), (0, 1, 2, 3), (2, 0, 1, 3),
+    (2, 0, 1, 3), (1, 3, 0, 2), (1, 2, 0, 3), (2, 0, 3, 1), (1, 0, 2, 3), (1, 0, 2, 3),
+    (0, 1, 2, 3), (1, 2, 0, 3), (2, 0, 1, 3), (1, 2, 0, 3),
 )
 PLAN_STEPS = (
-    96, 192, 32, 64, 97, 113, 160, 224, 193, 128, 98, 209, 0, 81, 114, 49, 177, 33, 99, 225, 161,
-    65, 145, 241, 1, 129, 82, 50, 194, 34, 178, 210, 115, 162, 17, 146, 130, 100, 226, 66, 2, 242,
-    51, 195, 83, 35, 179, 18, 147, 131, 227, 3, 116, 101, 163, 84, 211, 67, 243, 36, 180, 52, 19,
-    196, 228, 148, 132, 4, 117, 212, 164, 85, 102, 68, 181, 244, 37, 53, 20, 197, 149, 5, 133, 118,
-    213, 229, 165, 38, 86, 69, 182, 245, 198, 21, 150, 6, 134, 54, 119, 230, 122, 166, 70, 214, 39,
-    246, 183, 22, 186, 42, 103, 151, 87, 90, 199, 55, 106, 58, 135, 7, 154, 202, 231, 234, 10, 247,
-    167, 120, 71, 215, 218, 121, 250, 23, 40, 138, 41, 26, 184, 104, 152, 185, 105, 74, 153, 200,
-    56, 88, 57, 201, 89, 170, 8, 232, 136, 9, 137, 233, 216, 168, 248, 169, 217, 249, 24, 72, 73,
-    25,
+    0, 160, 128, 32, 96, 161, 64, 224, 1, 17, 177, 33, 49, 162, 97, 113, 145, 129, 81, 65, 192, 241,
+    178, 98, 34, 225, 163, 2, 146, 50, 114, 18, 66, 82, 242, 179, 209, 193, 130, 99, 3, 35, 226,
+    164, 115, 147, 83, 51, 67, 19, 243, 194, 210, 131, 36, 100, 4, 116, 227, 180, 165, 84, 20, 211,
+    195, 68, 101, 117, 148, 244, 132, 52, 166, 228, 181, 37, 5, 85, 21, 212, 196, 69, 102, 245, 53,
+    149, 133, 182, 6, 229, 38, 118, 22, 213, 197, 70, 246, 167, 86, 134, 230, 170, 54, 183, 150, 39,
+    214, 7, 23, 198, 71, 103, 119, 26, 42, 74, 247, 10, 186, 87, 135, 55, 231, 106, 250, 234, 90,
+    58, 122, 151, 215, 168, 199, 184, 169, 154, 218, 185, 24, 40, 120, 121, 41, 25, 202, 104, 248,
+    8, 249, 105, 9, 138, 136, 72, 88, 89, 137, 56, 232, 233, 73, 57, 216, 200, 152, 153, 201, 217,
 )
 
 
@@ -86,9 +85,24 @@
     return slots
 
 
-def permuted(index, order):
+def digits(flip, bits, bit):
+    if bits < 2:
+        return [bit(b) for b in range(bits)]
+    first, second = bit(0), bit(1)
+    change = flip * (second - first)
+    return [first + change, second - change] + [bit(b) for b in range(2, bits)]
+
+
+def weights(flip, bits):
+    if bits < 2:
+        return [2**b for b in range(bits)]
+    return [1 + flip, 2 - flip] + [2**b for b in range(2, bits)]
+
+
+def permuted(flip, index, order):
     bits = len(order)
-    return sum(((index // 2**b) % 2) * 2 ** (bits - 1 - at) for at, b in enumerate(order))
+    values = digits(flip, bits, lambda b: (index // 2**b) % 2)
+    return sum(values[b] * 2 ** (bits - 1 - at) for at, b in enumerate(order))
 
 
 def twiddles(no, lon_local, orders):
@@ -142,10 +156,10 @@
     modes = order_ref.shape[1]
 
     barrier = pltpu.get_barrier_semaphore()
-    partners = []
-    for b in range(bits):
-        mine = (me // 2**b) % 2
-        partners.append(me + (1 - 2 * mine) * 2**b)
+    flip = core % 2
+    my_bits = digits(flip, bits, lambda b: (me // 2**b) % 2)
+    scale_of = weights(flip, bits)
+    partners = [me + (1 - 2 * my_bits[b]) * scale_of[b] for b in range(bits)]
     peers = [lax.rem(core + i, no) for i in range(1, no)]
     for peer in peers:
         pl.semaphore_signal(barrier, inc=1, device_id=(me, peer), device_id_type=MESH)
@@ -268,7 +282,7 @@
     def region(g, k):
         base = 0
         for at in range(k):
-            base = base + ((me // 2 ** orders_of[g][at]) % 2) * (n >> (at + 1))
+            base = base + my_bits[orders_of[g][at]] * (n >> (at + 1))
         return base
 
     def analyse(u):
@@ -291,7 +305,7 @@
                 rows = slice(v * go, (v + 1) * go)
                 value = jnp.concatenate([real[rows], imag[rows]], 0).astype(BF16)
                 for j in range(blocks):
-                    to = permuted(i * blocks + j, orders_of[g])
+                    to = permuted(flip, i * blocks + j, orders_of[g])
                     part[g, to] = value[:, j * share : (j + 1) * share]
 
     reduce_copies = {}
@@ -300,7 +314,7 @@
     def send_reduce(g, k):
         h = n >> (k + 1)
         b = orders_of[g][k]
-        mine = (me // 2**b) % 2
+        mine = my_bits[b]
         copy = pltpu.make_async_remote_copy(
             src_ref=part.at[g, pl.ds(region(g, k) + (1 - mine) * h, h)],
             dst_ref=landed.at[g, pl.ds(n - (n >> k), h)],
@@ -377,7 +391,7 @@
         for i in range(degrees // width):
             first = i * width
             even, _ = parity(g * go, go, first)
-            pieces = [scaled[g, permuted(i * blocks + j, orders_of[g])] for j in range(blocks)]
+            pieces = [scaled[g, permuted(flip, i * blocks + j, orders_of[g])] for j in range(blocks)]
             stacked = stacked_of(pieces, jnp.where(even, 1.0, -1.0))
             total = lax.dot_general(
                 tab[g * rows_g : (g + 1) * rows_g, first : first + width], stacked, NT,
@@ -388,7 +402,7 @@
 
     def synthesise_half(g, late):
         order = orders_of[g]
-        mine = (me // 2 ** order[0]) % 2
+        mine = my_bits[order[0]]
         side = 1 - mine if late else mine
         half = n // 2
         quarter = half // 2
@@ -397,9 +411,9 @@
         for part_at in range(2):
             pieces, columns = [], []
             for i in range(part_at * quarter, (part_at + 1) * quarter):
-                block = side * 2 ** order[0]
+                block = side * scale_of[order[0]]
                 for at in range(1, bits):
-                    block = block + ((i >> (bits - 1 - at)) & 1) * 2 ** order[at]
+                    block = block + ((i >> (bits - 1 - at)) & 1) * scale_of[order[at]]
                 pieces.append(scaled[g, side * half + i])
                 start = pl.multiple_of(block * share, share)
                 columns.append(tab[g * rows_g : (g + 1) * rows_g, pl.ds(start, share)])

time: 50.9 us -> 50.4 us (level)
  no operation moved by 1% of the time
where the time goes in v6:
time: 50.4 us; the launch traced here: 50.2 us
  Pallas kernels  49.6 us (98%)
  between operations  0.64 us (1%)
    pallas_call x1, Pallas kernels, per_device(): pl.pallas_call(functools.partial(kernel, n, no), out_shape=(jax.ShapeDtyp...  47.8 us
    pallas_call x1, Pallas kernels, per_device(): pl.pallas_call(finish, out_shape=(jax.ShapeDtypeStruct(spectrum.shape, F3...  1.74 us

profile of v6, /device:TPU:1, one launch (start us, length us, event | category | flops | bytes accessed | tf_op | source)
XLA Modules:
  0.0 50.2 jit_solution(7176878678041796012)
XLA Ops:
  0.6 47.8 %shard_map.113 = (f32[2,256,128]{2,1,0:T(8,128)}, f32[2,8,2880]{2,1,0:T(8,128)}) custom-call(bf16[2,8,2880]{2,1,0:T(8,128)(2,1)} %press_hbm.1, bf16[2048,2048]{1,0:T(8,128)(2,1)} %bitcast.5, f32[1,128]{1,0:T(1,128)} %bitcast.8, f32[16,128]{1,0:T(8,128)} %bitcast.6, s32[1,512]{1,0:T(1,128)} %bitcast.7, s32[1,8]{1,0:T(1,128)} %bitcast.9, ...), custom_call_target="tpu_custom_call" | custom-call | tf_op jit(solution)/shard_map/pallas_call | solution.py:523
  48.5 1.7 %shard_map.114 = (f32[2,256,128]{2,1,0:T(8,128)}, f32[2,8,2880]{2,1,0:T(8,128)}) custom-call(f32[2,256,128]{2,1,0:T(8,128)} %get-tuple-element.4.half_spec, f32[2,8,2880]{2,1,0:T(8,128)} %get-tuple-element.5.half_field), custom_call_target="tpu_custom_call" | custom-call | tf_op jit(solution)/shard_map/pallas_call | solution.py:561

commit v7 on v6

--- a/solution.py
+++ b/solution.py
@@ -120,7 +120,7 @@
     starts = (lon_local * np.arange(no)[:, None] + LANES * np.arange(blocks)).reshape(-1)
     cos, sin = turn(starts)
     fine = np.concatenate([high, low], 0)
-    return fine, cos.astype(np.float32), sin.astype(np.float32), np.ascontiguousarray(fine.T)
+    return fine, cos.astype(np.float32), sin.astype(np.float32), np.ascontiguousarray(high.T)
 
 
 def kernel(
@@ -471,8 +471,7 @@
         rows = slice(q * both, (q + 1) * both)
         rotated[rows, :modes] = (real * cq - imag * sq).astype(BF16)
         rotated[rows, modes:] = (-real * sq - imag * cq).astype(BF16)
-    parts = jnp.dot(rotated[...], back[...], preferred_element_type=F32)
-    field = parts[:, :LANES] + parts[:, LANES:]
+    field = jnp.dot(rotated[...], back[...], preferred_element_type=F32)
     for q in range(turns):
         first = q * LANES
         count = min(LANES, lon_local - first)

time: 50.4 us -> 50.4 us (level)
  no operation moved by 1% of the time
where the time goes in v7:
time: 50.4 us; the launch traced here: 50.2 us
  Pallas kernels  49.6 us (98%)
  between operations  0.64 us (1%)
    pallas_call x1, Pallas kernels, per_device(): pl.pallas_call(functools.partial(kernel, n, no), out_shape=(jax.ShapeDtyp...  47.8 us
    pallas_call x1, Pallas kernels, per_device(): pl.pallas_call(finish, out_shape=(jax.ShapeDtypeStruct(spectrum.shape, F3...  1.74 us

profile of v7, /device:TPU:1, one launch (start us, length us, event | category | flops | bytes accessed | tf_op | source)
XLA Modules:
  0.0 50.2 jit_solution(10277828723585823720)
XLA Ops:
  0.6 47.8 %shard_map.113 = (f32[2,256,128]{2,1,0:T(8,128)}, f32[2,8,2880]{2,1,0:T(8,128)}) custom-call(bf16[2,8,2880]{2,1,0:T(8,128)(2,1)} %press_hbm.1, bf16[2048,2048]{1,0:T(8,128)(2,1)} %bitcast.5, f32[1,128]{1,0:T(1,128)} %bitcast.8, f32[16,128]{1,0:T(8,128)} %bitcast.6, s32[1,512]{1,0:T(1,128)} %bitcast.7, s32[1,8]{1,0:T(1,128)} %bitcast.9, ...), custom_call_target="tpu_custom_call" | custom-call | tf_op jit(solution)/shard_map/pallas_call | solution.py:522
  48.5 1.7 %shard_map.114 = (f32[2,256,128]{2,1,0:T(8,128)}, f32[2,8,2880]{2,1,0:T(8,128)}) custom-call(f32[2,256,128]{2,1,0:T(8,128)} %get-tuple-element.4.half_spec, f32[2,8,2880]{2,1,0:T(8,128)} %get-tuple-element.5.half_field), custom_call_target="tpu_custom_call" | custom-call | tf_op jit(solution)/shard_map/pallas_call | solution.py:560
